TPU v7x, 64 devices: a 2x2x8 block of a 4x4x8 slice. The times are simulated.
64 devices in a mesh: dp: 4 (over x, y), ep: 16 (over z, core).
Axes of the slice: x: 2, y: 2, z: 8, core: 2. Of those that a mesh axis runs over, the one named last changes fastest.
The devices are a block of a 4x4x8 slice.
Arguments:
- resid_in: bfloat16 [4096, 2560], P(('dp', 'ep')), parts along dimension 0
- expert_ids: int32 [4096, 6], P(('dp', 'ep')), parts along dimension 0
- priority: int32 [4096, 6], P(('dp', 'ep')), parts along dimension 0
- norm_gain: float32 [2560], replicated
- router_w: bfloat16 [2560, 64], replicated
- shared_w1: bfloat16 [2560, 3072], replicated
- shared_w3: bfloat16 [2560, 3072], replicated
- shared_w2: bfloat16 [3072, 2560], replicated
- expert_w1: bfloat16 [64, 2560, 1536], P('ep')
- expert_w3: bfloat16 [64, 2560, 1536], P('ep')
- expert_w2: bfloat16 [64, 1536, 2560], P('ep')
Outputs:
- output: bfloat16 [4096, 2560], P(('dp', 'ep')), parts along dimension 0
There are 4 independent parts. A program takes and returns all parts, laid end to end along the dimension named above; an argument that names none is the same for every part.
All inputs are finite; a program needn't handle non-finite values.
Results may differ from a plain program's by a relative error of at most 0.00678726.
Values are sent between devices in bfloat16 or wider.
A program may use at most 768 MiB of HBM per device.

v0:
```python
import jax
import jax.numpy as jnp
from jax import lax
from jax.sharding import PartitionSpec as P

NORM_EPS = 1e-6
ROUTE_SCALE = 16.0


def rms_norm(resid_in, norm_gain):
    resid32 = resid_in.astype(jnp.float32)
    inv_rms = lax.rsqrt(jnp.mean(resid32 * resid32, axis=1, keepdims=True) + NORM_EPS)
    return (resid32 * inv_rms * norm_gain).astype(jnp.bfloat16)


def gate_values(normed, router_w, expert_ids):
    gate_probs = jax.nn.softmax(jnp.dot(normed, router_w, preferred_element_type=jnp.float32), axis=1)
    return ROUTE_SCALE * jnp.take_along_axis(gate_probs, expert_ids, axis=1)


def swiglu_ffn(normed, w_gate, w_up, w_down):
    up_a = jnp.dot(normed, w_gate, preferred_element_type=jnp.float32)
    up_b = jnp.dot(normed, w_up, preferred_element_type=jnp.float32)
    hidden_act = (jax.nn.silu(up_a) * up_b).astype(jnp.bfloat16)
    return jnp.dot(hidden_act, w_down, preferred_element_type=jnp.float32).astype(jnp.bfloat16)


def grouped_ffn(row_inputs, group_sizes, slot_valid, expert_w1, expert_w3, expert_w2):
    up_a = lax.ragged_dot(row_inputs, expert_w1, group_sizes, preferred_element_type=jnp.float32)
    up_b = lax.ragged_dot(row_inputs, expert_w3, group_sizes, preferred_element_type=jnp.float32)
    hidden_act = (jax.nn.silu(up_a) * up_b).astype(jnp.bfloat16)
    expert_out = lax.ragged_dot(hidden_act, expert_w2, group_sizes, preferred_element_type=jnp.float32).astype(jnp.bfloat16)
    return jnp.where(slot_valid[:, None], expert_out.astype(jnp.float32), 0.0)


def local_keep(flat_ids, prio_flat, local_experts, capacity, my_index):
    n_assign = flat_ids.shape[0]
    mine_int = (flat_ids // local_experts == my_index).astype(jnp.int32)
    by_rank = jnp.zeros((n_assign,), jnp.int32).at[prio_flat].set(mine_int)
    before = jnp.cumsum(by_rank) - by_rank
    return (mine_int > 0) & (before[prio_flat] < capacity)


def slot_layout(flat_ids, mine_kept, local_experts, capacity, my_index):
    n_assign = flat_ids.shape[0]
    local_e = flat_ids - my_index * local_experts
    sort_key = jnp.where(mine_kept, local_e, local_experts) * n_assign + jnp.arange(n_assign, dtype=jnp.int32)
    slot_order = jnp.argsort(sort_key)[:capacity]
    group_sizes = jax.ops.segment_sum(mine_kept.astype(jnp.int32), jnp.where(mine_kept, local_e, 0), num_segments=local_experts)
    return slot_order, group_sizes, mine_kept[slot_order]


def solution(mesh):
    ep_size = mesh.shape['ep']
    tok_spec = P(('dp', 'ep'))
    expert_spec = P('ep')

    def device_fn(resid_in, expert_ids, priority, norm_gain, router_w, shared_w1, shared_w3, shared_w2, expert_w1, expert_w3, expert_w2):
        tok_local = resid_in.shape[0]
        top_k = expert_ids.shape[1]
        local_experts = expert_w1.shape[0]
        capacity = tok_local * top_k
        my_index = lax.axis_index('ep')
        normed = rms_norm(resid_in, norm_gain)
        gate_vals = gate_values(normed, router_w, expert_ids)
        shared_out = swiglu_ffn(normed, shared_w1, shared_w3, shared_w2)
        all_ids = lax.all_gather(expert_ids, 'ep', tiled=True).reshape(-1)
        all_prio = lax.all_gather(priority, 'ep', tiled=True).reshape(-1)
        all_gates = lax.all_gather(gate_vals, 'ep', tiled=True).reshape(-1)
        all_normed = lax.all_gather(normed, 'ep', tiled=True)
        mine_kept = local_keep(all_ids, all_prio, local_experts, capacity, my_index)
        slot_order, group_sizes, slot_valid = slot_layout(all_ids, mine_kept, local_experts, capacity, my_index)
        tok_of = slot_order // top_k
        expert_out = grouped_ffn(all_normed[tok_of], group_sizes, slot_valid, expert_w1, expert_w3, expert_w2)
        weighted = expert_out * all_gates[slot_order][:, None]
        token_sums = jax.ops.segment_sum(weighted, tok_of, num_segments=tok_local * ep_size)
        routed = lax.psum_scatter(token_sums, 'ep', scatter_dimension=0, tiled=True)
        out_sum = resid_in.astype(jnp.float32) + shared_out.astype(jnp.float32) + routed
        return out_sum.astype(jnp.bfloat16)

    return jax.shard_map(device_fn, mesh=mesh, in_specs=(tok_spec, tok_spec, tok_spec, P(), P(), P(), P(), P(), expert_spec, expert_spec, expert_spec), out_specs=tok_spec, check_vma=False)
```

profile of v0, /device:TPU:21, one launch (start us, length us, event | category | flops | bytes accessed | tf_op | source)
XLA Modules:
  0.0 358.5 jit_solution(17601450980155091797)
XLA Ops:
  6.6 1.2 fusion.14
  7.8 1.9 fusion.16
  9.7 23.0 %all-gather = s32[16,64,6]{1,2,0:T(8,128)S(1)} all-gather(s32[1,64,6]{1,2,0:T(8,128)} %bitcast.20), channel_id=1, replica_groups=mesh['dp'=4,'ep'=16] {'ep'}, dimensions={0}, use_global_device_ids=true | all-gather | bytes 26112 | tf_op jit(solution)/shard_map/all_gather | solution.py:67
  33.3 0.4 reshape.182
  33.7 15.0 %all-gather.1 = s32[16,64,6]{1,2,0:T(8,128)S(1)} all-gather(s32[1,64,6]{1,2,0:T(8,128)} %bitcast.22), channel_id=1, replica_groups=mesh['dp'=4,'ep'=16] {'ep'}, dimensions={0}, use_global_device_ids=true | all-gather | bytes 26112 | tf_op jit(solution)/shard_map/all_gather | solution.py:68
  49.0 0.4 reshape.179
  49.4 23.0 %scatter_custom_fusion = s32[6144]{0:T(1024)S(1)} fusion(s32[6144]{0:T(1024)S(1)} %bitcast.18, s32[6144]{0:T(1024)S(1)} %fusion.23, s32[]{:T(128)} %constant.39.clone.1), kind=kCustom, calls=%fused_computation.56 | custom fusion | bytes 24580 | tf_op jit(solution)/shard_map/scatter | solution.py:39
  73.1 34.3 %gather_fusion = s32[6144]{0:T(1024)S(1)} fusion(s32[6144]{0:T(1024)S(1)} %bitcast_subtract_fusion, s32[6144]{0:T(1024)S(1)} %broadcast_clamp_fusion), kind=kCustom, calls=%fused_computation | custom fusion | bytes 73728 | tf_op jit(solution)/shard_map/gather | solution.py:41
  107.6 43.4 %scatter_custom_fusion.1 = s32[4]{0:T(128)} fusion(s32[6144]{0:T(1024)S(1)} %bitcast.21, s32[6144]{0:T(1024)S(1)} %get-tuple-element.21, s32[]{:T(128)} %constant.39.clone.1), kind=kCustom, calls=%fused_computation.70 | custom fusion | flops 6144 | bytes 20 | tf_op jit(solution)/shard_map/scatter-add | solution.py:49
  151.0 1.4 ragged-dot-metadata
  152.4 6.7 %sort.17 = (s32[6144]{0:T(1024)}, s32[6144]{0:T(1024)S(1)}) sort(s32[6144]{0:T(1024)S(1)} %iota_add_fusion, s32[6144]{0:T(1024)S(1)} %iota.8), dimensions={0}, to_apply=%region_4.5 | sort | flops 79872 | bytes 98304 | tf_op jit(solution)/shard_map/jit(argsort)/sort | solution.py:48
  159.2 2.8 gather_fusion.1
  162.7 3.0 gather_fusion.4
  165.9 16.2 %all-gather.2 = f32[16,64,6]{1,2,0:T(8,128)S(1)} all-gather(f32[1,64,6]{1,2,0:T(8,128)S(1)} %multiply_bitcast_fusion), channel_id=1, replica_groups=mesh['dp'=4,'ep'=16] {'ep'}, dimensions={0}, use_global_device_ids=true | all-gather | bytes 26112 | tf_op jit(solution)/shard_map/all_gather | solution.py:69
  182.6 2.5 gather_fusion.3
  185.2 9.0 %gather_fusion.2 = bf16[384,2560]{1,0:T(8,128)(2,1)} fusion(bf16[1024,2560]{1,0:T(8,128)(2,1)} %all-gather.5.cloned.1.call-done, s32[1024]{0:T(1024)S(1)} %pad_clamp_fusion), kind=kCustom, calls=%fused_computation.2 | custom fusion | bytes 3933696 | tf_op jit(solution)/shard_map/gather | solution.py:74
  194.3 16.9 %ragged-dot-none.2 = f32[384,1536]{1,0:T(8,128)} custom-call(s32[1]{0:T(128)} %get-tuple-element.7, s32[5]{0:T(128)} %get-tuple-element.8, s32[6]{0:T(128)} %get-tuple-element.9, s32[6]{0:T(128)} %get-tuple-element.10, s32[1]{0:T(128)} %get-tuple-element.7, bf16[384,2560]{1,0:T(8,128)(2,1)} %gather_fusion.2, bf16[4,2560,1536]{2,1,0:T(8,128)(2,1)} %param.19), custom_call_target="tpu_custom_call" | custom-call | flops 3019898880 | bytes 35782672 | tf_op jit(solution)/shard_map/ragged_dot_general/ragged-dot-none
  211.2 17.1 %ragged-dot-none.1 = f32[384,1536]{1,0:T(8,128)} custom-call(s32[1]{0:T(128)} %get-tuple-element.7, s32[5]{0:T(128)} %get-tuple-element.8, s32[6]{0:T(128)} %get-tuple-element.9, s32[6]{0:T(128)} %get-tuple-element.10, s32[1]{0:T(128)} %get-tuple-element.7, bf16[384,2560]{1,0:T(8,128)(2,1)} %gather_fusion.2, bf16[4,2560,1536]{2,1,0:T(8,128)(2,1)} %param.20), custom_call_target="tpu_custom_call" | custom-call | flops 3019898880 | bytes 35782672 | tf_op jit(solution)/shard_map/ragged_dot_general/ragged-dot-none
  228.2 3.4 multiply_convert_fusion
  231.6 17.2 %ragged-dot-none = f32[384,2560]{1,0:T(8,128)} custom-call(s32[1]{0:T(128)} %get-tuple-element.7, s32[5]{0:T(128)} %get-tuple-element.8, s32[6]{0:T(128)} %get-tuple-element.9, s32[6]{0:T(128)} %get-tuple-element.10, s32[1]{0:T(128)} %get-tuple-element.7, bf16[384,1536]{1,0:T(8,128)(2,1)} %multiply_convert_fusion, bf16[4,1536,2560]{2,1,0:T(8,128)(2,1)} %param.21), custom_call_target="tpu_custom_call" | custom-call | flops 3019898880 | bytes 36569104 | tf_op jit(solution)/shard_map/ragged_dot_general/ragged-dot-none
  248.9 12.7 %scatter_custom_fusion.2 = f32[1024,2560]{1,0:T(8,128)} fusion(s32[384]{0:T(512)S(1)} %get-tuple-element.20, f32[]{:T(128)} %constant.24.clone.1, f32[384]{0:T(512)S(1)} %gather_fusion.3, f32[384,2560]{1,0:T(8,128)} %ragged-dot-none, pred[384]{0:T(512)(128)(4,1)S(1)} %gather_fusion.1), kind=kCustom, calls=%fused_computation.8 | custom fusion | flops 4915200 | bytes 14421504 | tf_op jit(solution)/shard_map/scatter-add | solution.py:76
  261.6 8.4 %fusion.34 = f32[64,3072]{1,0:T(8,128)S(1)} fusion(bf16[2560,3072]{1,0:T(8,128)(2,1)} %param.16, bf16[64,2560]{1,0:T(8,128)(2,1)S(1)} %copy-done.3, f32[2560]{0:T(1024)S(1)} %copy-done.4, f32[64]{0:T(128)S(1)} %add_rsqrt_fusion), kind=kOutput, calls=%fused_computation.74 | convolution fusion | flops 1007288320 | bytes 16853248 | tf_op jit(solution)/shard_map/dot_general | solution.py:22
  270.0 65.2 %reduce-scatter.2.cloned.1.call-done = f32[64,2560]{1,0:T(8,128)} async-done(((f32[1024,2560]{1,0:T(8,128)}), f32[64,2560]{1,0:T(8,128)}) %reduce-scatter.2.cloned.1.call-update) | async-done | bytes 655376 | tf_op jit(solution)/shard_map/reduce_scatter | solution.py:77
  335.2 16.5 %fusion.8 = bf16[64,2560]{1,0:T(8,128)(2,1)} fusion(f32[64,2560]{1,0:T(8,128)} %reduce-scatter.2.cloned.1.call-done, bf16[3072,2560]{1,0:T(8,128)(2,1)} %param.18, bf16[64,2560]{1,0:T(8,128)(2,1)S(1)} %copy-done.3, bf16[2560,3072]{1,0:T(8,128)(2,1)} %param.17, f32[64,3072]{1,0:T(8,128)S(1)} %fusion.34, f32[2560]{0:T(1024)S(1)} %copy-done.4, ...), kind=kOutput, calls=%fused_computation.18 | convolution fusion | flops 2016083968 | bytes 33564928 | tf_op jit(solution)/shard_map/dot_general | solution.py:25
  (47 shorter events, 3.4 us)
Async XLA Ops:
  6.5 155.7 %copy-start = (bf16[2560,64]{0,1:T(8,128)(2,1)S(1)}, bf16[2560,64]{0,1:T(8,128)(2,1)}, u32[]{:S(2)}) copy-start(bf16[2560,64]{0,1:T(8,128)(2,1)} %param.15) | copy-start | bytes 983044
  6.6 178.7 %all-gather.5.cloned.1.call-start = ((), (), s32[]{:S(2)}) async-start(), calls=%async_computation.1 | async-start | bytes 5570560 | tf_op jit(solution)/shard_map/all_gather | solution.py:70
  9.7 325.6 %reduce-scatter.2.cloned.1.call-start = ((), (), s32[]{:S(2)}) async-start(), calls=%async_computation.2 | async-start | bytes 11141120 | tf_op jit(solution)/shard_map/reduce_scatter | solution.py:77
  73.1 88.9 %copy-start.5 = (s32[64,6]{0,1:T(8,128)S(1)}, s32[64,6]{0,1:T(8,128)}, u32[]{:S(2)}) copy-start(s32[64,6]{0,1:T(8,128)} %param.12) | copy-start | bytes 4612
  73.1 89.2 %copy-start.3 = (bf16[64,2560]{1,0:T(8,128)(2,1)S(1)}, bf16[64,2560]{1,0:T(8,128)(2,1)}, u32[]{:S(2)}) copy-start(bf16[64,2560]{1,0:T(8,128)(2,1)} %param.11) | copy-start | bytes 983044
  73.1 89.2 %copy-start.4 = (f32[2560]{0:T(1024)S(1)}, f32[2560]{0:T(1024)}, u32[]{:S(2)}) copy-start(f32[2560]{0:T(1024)} %param.14) | copy-start | bytes 30724
  211.2 17.1 %copy-start.2 = (f32[384,1536]{1,0:T(8,128)S(1)}, f32[384,1536]{1,0:T(8,128)}, u32[]{:S(2)}) copy-start(f32[384,1536]{1,0:T(8,128)} %ragged-dot-none.2) | copy-start | bytes 7077892
  335.2 16.5 %copy-start.1 = (bf16[2560,64]{0,1:T(8,128)(2,1)S(1)}, bf16[2560,64]{0,1:T(8,128)(2,1)}, u32[]{:S(2)}) copy-start(bf16[2560,64]{0,1:T(8,128)(2,1)} %param.15) | copy-start | bytes 983044
Sparse Core Ops, SparseCore 0:
  9.8 45.4 all-gather.4
  261.7 73.4 reduce-scatter.1
where the time goes:
time: 361 us; the launch traced here: 359 us
  local copies, waits for them, and re-layouts  77.4 us (21%)
  other arithmetic  70.1 us (19%)
  waiting for transfers between devices  65.4 us (18%)
  blocking collectives  54.2 us (15%)
  Pallas kernels  52.6 us (15%)
  matrix products  25.2 us (7%)
  between operations  13.7 us (4%)
    reduce_scatter x1, waiting for transfers between devices, device_fn(): routed = lax.psum_scatter(token_sums, 'ep', scatter_dimension=0, tiled=True)  65.2 us
    another operation x3, Pallas kernels  51.2 us
    scatter-add x1, other arithmetic, slot_layout(): jax.ops.segment_sum(mine_kept.astype(jnp.int32), jnp.where(mine_kept, loc...  43.4 us
    gather x1, local copies, waits for them, and re-layouts, local_keep(): return (mine_int > 0) & (before[prio_flat] < capacity)  34.3 us
    scatter x1, local copies, waits for them, and re-layouts, local_keep(): by_rank = jnp.zeros((n_assign,), jnp.int32).at[prio_flat].set(mine_int)  23 us
    all_gather x1, blocking collectives, device_fn(): all_ids = lax.all_gather(expert_ids, 'ep', tiled=True).reshape(-1)  23 us
    dot_general x1, matrix products, swiglu_ffn(): jnp.dot(hidden_act, w_down, preferred_element_type=jnp.float32)  16.5 us
    all_gather x1, blocking collectives, device_fn(): all_gates = lax.all_gather(gate_vals, 'ep', tiled=True).reshape(-1)  16.2 us
  transfers between devices with their start and end apart: 2, of which 1 were waited for; matrix products, arithmetic and copies ran while one was open for 36% of the time, Pallas kernels for 0%

commit v1 on v0

v1 whole, which is shorter than its diff:
```python
import functools

import jax
import jax.numpy as jnp
from jax import lax
from jax.experimental import pallas as pl
from jax.experimental.pallas import tpu as pltpu
from jax.sharding import PartitionSpec as P

NORM_EPS = 1e-6
ROUTE_SCALE = 16.0
KC = 256
TILE = 128
KPAD = 8
F32 = jnp.float32
BF16 = jnp.bfloat16


def dot(a, b):
    return jnp.dot(a, b, preferred_element_type=F32)


def ring_place(dm):
    n = dm.n_chip
    me = lax.axis_index("ep")
    chip = me // 2
    core = me - 2 * chip
    d = 1 - 2 * core

    def at(h):
        return lax.rem(chip + h * d + 2 * n, n)

    return me, chip, core, at, 2 * chip + 1 - core, 2 * at(1) + core, 2 * at(-1) + core


def rcopy(src, dst, ssem, rsem, dev):
    return pltpu.make_async_remote_copy(src_ref=src, dst_ref=dst, send_sem=ssem, recv_sem=rsem,
                                        device_id={"ep": dev}, device_id_type=pl.DeviceIdType.MESH)


def entry_barrier(devs):
    barrier = pltpu.get_barrier_semaphore()
    for dev in devs:
        pl.semaphore_signal(barrier, inc=1, device_id={"ep": dev}, device_id_type=pl.DeviceIdType.MESH)
    pl.semaphore_wait(barrier, len(devs))


def cond(static, pred, fn):
    if static:
        if pred:
            fn()
    else:
        pl.when(pred)(fn)


def start(copies):
    for c in copies:
        c.start()


def wait(copies):
    for c in copies:
        c.wait()


def gather_kernel(dm, b_ref, info_ref, X, PG, WC, TE,
                  I, SLT, GLT, lsem, xs_ring, xr_ring, xs_d2d, xr_d2d, is_ring, ir_ring, is_d2d, ir_d2d, p_s, p_r):
    n = dm.n_chip
    hops = n // 2
    tok = dm.tok
    crows = 2 * tok
    nj = dm.nj
    off = hops + 1
    slots = dm.slots
    n_tiles = slots // TILE
    group = n * crows
    me, chip, core, at, partner, down, up = ring_place(dm)
    half = pl.ds(pl.multiple_of(core * tok, tok), tok)
    entry_barrier((partner, down, up))

    own_x = X.at[:, chip, half, :]
    own_i = I.at[chip, core]
    first = [rcopy(b_ref, own_x, p_s.at[0], p_r.at[0], partner), rcopy(info_ref, own_i, p_s.at[1], p_r.at[1], partner)]
    start(first)
    local = [pltpu.make_async_copy(b_ref, own_x, lsem.at[0]), pltpu.make_async_copy(info_ref, own_i, lsem.at[1])]
    start(local)
    wait(local)
    for c in first:
        c.wait_recv()

    def x_block(j, h, rows_half):
        return X.at[j, at(-h), half, :] if rows_half else X.at[j, at(-h)]

    def x_ring(j, h):
        blk = x_block(j, h, h + 1 == hops)
        return rcopy(blk, blk, xs_ring.at[h, j], xr_ring.at[h, j], down)

    def x_ring_in(j, h):
        blk = x_block(j, h, h == hops)
        return rcopy(blk, blk, xs_ring.at[h - 1, j], xr_ring.at[h - 1, j], down)

    def x_d2d(j, h):
        blk = x_block(j, h, h == hops)
        return rcopy(blk, blk, xs_d2d.at[h - 1, j], xr_d2d.at[h - 1, j], partner)

    def x_d2d_in(j, h):
        blk = X.at[j, at(h), pl.ds(pl.multiple_of((1 - core) * tok, tok), tok), :] if h == hops else X.at[j, at(h)]
        return rcopy(blk, blk, xs_d2d.at[h - 1, j], xr_d2d.at[h - 1, j], partner)

    def comm(s, static):
        def hop(h):
            j = s - h

            def run():
                if h > 0:
                    x_ring_in(j, h).wait_recv()
                if h < hops:
                    x_ring(j, h).start()
                if h > 0:
                    x_d2d(j, h).start()
            cond(static, (j < nj and j >= 0) if static else (j < nj), run)
        hop(0)
        for h in range(hops, 0, -1):
            hop(h)

    def i_block(h, rows_half, sign=-1, c=None):
        return I.at[at(sign * h), core if c is None else c] if rows_half else I.at[at(sign * h)]

    def comm_info(h):
        if h > 0:
            blk = i_block(h, h == hops)
            rcopy(blk, blk, is_ring.at[h - 1], ir_ring.at[h - 1], down).wait_recv()
        if h < hops:
            blk = i_block(h, h + 1 == hops)
            rcopy(blk, blk, is_ring.at[h], ir_ring.at[h], down).start()
        if h > 0:
            blk = i_block(h, h == hops)
            rcopy(blk, blk, is_d2d.at[h - 1], ir_d2d.at[h - 1], partner).start()

    for s in range(off):
        comm_info(s)
        comm(s, True)

    for h in range(1, hops + 1):
        blk = i_block(h, h == hops, 1, 1 - core)
        rcopy(blk, blk, is_d2d.at[h - 1], ir_d2d.at[h - 1], partner).wait_recv()

    lanes = crows
    nr = n * KPAD

    def field(i):
        rows = pl.ds(i * KPAD, KPAD)
        return (I[:, 0, rows, :] + I[:, 1, rows, :]).reshape(nr, lanes)

    mine_e = field(0) - (me * dm.local_e).astype(F32)
    prio = field(1)
    gate = field(2)
    mine = (mine_e >= 0) & (mine_e < dm.local_e)
    key = jnp.where(mine, prio, 1e9)
    cut = jnp.zeros((1, 1), F32)
    bit = 1 << (group * dm.top_k).bit_length()
    while bit >= 1:
        cand = cut + float(bit)
        cnt = jnp.sum(jnp.where(key < cand, 1.0, 0.0), keepdims=True)
        cut = jnp.where(cnt <= float(dm.capacity), cand, cut)
        bit //= 2
    kept = key < cut
    masks = [jnp.where(kept & (mine_e == float(e)), 1.0, 0.0) for e in range(dm.local_e)]
    stack = jnp.concatenate(masks, axis=0)
    li = lax.broadcasted_iota(jnp.int32, (lanes, lanes), 0)
    lj = lax.broadcasted_iota(jnp.int32, (lanes, lanes), 1)
    upper = jnp.where(li <= lj, 1.0, 0.0).astype(BF16)
    inrow = dot(stack.astype(BF16), upper)
    total_rows = dm.local_e * nr
    rowtot = jnp.broadcast_to(inrow[:, lanes - 1:lanes], (total_rows, lanes))
    ri = lax.broadcasted_iota(jnp.int32, (total_rows, total_rows), 0)
    rj = lax.broadcasted_iota(jnp.int32, (total_rows, total_rows), 1)
    lower = jnp.where((ri > rj) & (ri // nr == rj // nr), 1.0, 0.0).astype(BF16)
    before = dot(lower, rowtot.astype(BF16))
    slot_of = jnp.full((nr, lanes), -1.0, F32)
    base = jnp.zeros((1, lanes), F32)
    bound = jnp.int32(0)
    bounds = []
    for e in range(dm.local_e):
        rows = slice(e * nr, (e + 1) * nr)
        pos = base + before[rows] + inrow[rows] - 1.0
        slot_of = jnp.where(masks[e] > 0.5, pos, slot_of)
        last = (e + 1) * nr - 1
        count = before[last:last + 1] + rowtot[last:last + 1]
        base = base + jnp.floor((count + (TILE - 1.0)) * (1.0 / TILE)) * TILE
        count_i = jnp.sum(jnp.where(kept & (mine_e == float(e)), 1, 0))
        bound = bound + (count_i + (TILE - 1)) // TILE
        bounds.append(bound)
    tile_e = [sum(jnp.where(bounds[e] <= i, 1, 0) for e in range(dm.local_e - 1)) for i in range(n_tiles)]

    slot_t = slot_of.T
    gate_t = gate.T
    for c in range(n):
        SLT[c] = slot_t[:, c * KPAD:(c + 1) * KPAD]
        GLT[c] = gate_t[:, c * KPAD:(c + 1) * KPAD]
        for r in range(n_tiles):
            srow = (lax.broadcasted_iota(jnp.int32, (TILE, lanes), 0) + r * TILE).astype(F32)
            hit = jnp.zeros((TILE, lanes), F32)
            for k in range(dm.top_k):
                hit = jnp.where(slot_of[c * KPAD + k:c * KPAD + k + 1] == srow, 1.0, hit)
            PG[pl.ds(r * TILE, TILE), pl.ds(c * lanes, lanes)] = hit.astype(BF16)

    for i in range(n_tiles):
        TE[i] = tile_e[i]

    def combine_rows(c):
        sl = SLT[c]
        gl = GLT[c]
        rows = pl.ds(pl.multiple_of(c * crows, crows), crows)
        for p in range(slots // KC):
            scol = (lax.broadcasted_iota(jnp.int32, (crows, KC), 1) + p * KC).astype(F32)
            w = jnp.zeros((crows, KC), F32)
            for k in range(dm.top_k):
                w = jnp.where(sl[:, k:k + 1] == scol, gl[:, k:k + 1], w)
            for i in range(3):
                part = w.astype(BF16)
                WC[rows, pl.ds(i * slots + p * KC, KC)] = part
                w = w - part.astype(F32)

    def step(j, carry):
        comm(j + off, False)

        @pl.when(j < n)
        def _():
            combine_rows(j)
        return carry

    lax.fori_loop(0, nj - 1, step, 0)
    for c in range(nj - 1, n):
        combine_rows(c)

    def arrive(j, carry):
        for h in range(1, hops + 1):
            x_d2d_in(j, h).wait_recv()
        return carry

    lax.fori_loop(0, nj, arrive, 0)
    for c in first:
        c.wait_send()
    for h in range(hops):
        blk = i_block(h, h + 1 == hops)
        rcopy(blk, blk, is_ring.at[h], ir_ring.at[h], down).wait_send()
        blk = i_block(h + 1, h + 1 == hops)
        rcopy(blk, blk, is_d2d.at[h], ir_d2d.at[h], partner).wait_send()

    def drain(j, carry):
        for h in range(hops):
            x_ring(j, h).wait_send()
            x_d2d(j, h + 1).wait_send()
        return carry

    lax.fori_loop(0, nj, drain, 0)


def up_kernel(dm, te_ref, x_ref, pg_ref, w1_ref, w3_ref, h_ref, acc_ref):
    nt = dm.ff // KC
    j = pl.program_id(0)

    @pl.when(j == 0)
    def _():
        acc_ref[...] = jnp.zeros(acc_ref.shape, F32)

    xg = dot(pg_ref[...], x_ref[0].reshape(pg_ref.shape[1], KC)).astype(BF16)
    for i in range(dm.slots // TILE):
        xi = xg[i * TILE:(i + 1) * TILE]
        for m, w_ref in enumerate((w1_ref, w3_ref)):
            for c in range(nt):
                rows = pl.ds((m * nt + c) * dm.slots + i * TILE, TILE)
                acc_ref[rows, :] += dot(xi, w_ref[te_ref[i], :, pl.ds(c * KC, KC)])

    @pl.when(j == pl.num_programs(0) - 1)
    def _():
        for i in range(dm.slots // TILE):
            for c in range(nt):
                a = acc_ref[pl.ds(c * dm.slots + i * TILE, TILE), :]
                g = acc_ref[pl.ds((nt + c) * dm.slots + i * TILE, TILE), :]
                h_ref[pl.ds(i * TILE, TILE), pl.ds(c * KC, KC)] = (jax.nn.silu(a) * g).astype(BF16)


def down_kernel(dm, H, WC, TE, shared_ref, resid_ref, ew2, out_ref,
                BIG, V2A, V2B, E3, PR, RR, FR, vsem, qs, qr, rs, rr, fs, fr):
    n = dm.n_chip
    hops = n // 2
    tok = dm.tok
    crows = 2 * tok
    nj = dm.nj
    slots = dm.slots
    n_tiles = slots // TILE
    group = n * crows
    me, chip, core, at, partner, down, up = ring_place(dm)
    V2 = (V2A, V2B)

    def down_copies(j, slot):
        cols = pl.ds(pl.multiple_of(j * KC, KC), KC)
        return [pltpu.make_async_copy(ew2.at[:, :, cols], V2[slot], vsem.at[slot])]

    start(down_copies(0, 0))
    start(down_copies(1, 1))
    entry_barrier((partner, down, up))

    pr_off = [448, 0, 128, 256, 384]
    assert crows == 128 and hops == 4

    def dblk(j, dest, row, size):
        return pl.ds(pl.multiple_of(j * group + dest * crows + row, tok), size)

    def q_copy(j, h):
        if h == 0:
            src, size = BIG.at[dblk(j, chip, (1 - core) * tok, tok), :], tok
        elif h == hops:
            src, size = BIG.at[dblk(j, at(-h), (1 - core) * tok, tok), :], tok
        else:
            src, size = BIG.at[dblk(j, at(-h), 0, crows), :], crows
        return rcopy(src, PR.at[j, pl.ds(pr_off[h], size), :], qs.at[h, j], qr.at[h, j], partner)

    rr_off = [0, 64, 192, 320]

    def r_copy(j, g):
        h = hops - g
        src, size = (BIG.at[dblk(j, at(h), core * tok, tok), :], tok) if g == 0 else (BIG.at[dblk(j, at(h), 0, crows), :], crows)
        return rcopy(src, RR.at[j, pl.ds(rr_off[g], size), :], rs.at[g, j], rr.at[g, j], down)

    def f_copy(j):
        return rcopy(RR.at[j, pl.ds(pl.multiple_of(rr_off[hops - 1] + (1 - core) * tok, tok), tok), :], FR.at[j], fs.at[j], fr.at[j], partner)

    def finish(j):
        q_copy(j, 0).wait_recv()
        f_copy(j).wait_recv()
        cols = pl.ds(pl.multiple_of(j * KC, KC), KC)
        routed = BIG[dblk(j, chip, core * tok, tok), :] + PR[j, pl.ds(pr_off[0], tok), :]
        routed = routed + RR[j, pl.ds(pl.multiple_of(rr_off[hops - 1] + core * tok, tok), tok), :] + FR[j]
        out_ref[:, cols] = (resid_ref[:, cols].astype(F32) + shared_ref[:, cols].astype(F32) + routed).astype(BF16)

    def turn(j):
        r_copy(j, hops - 1).wait_recv()
        f_copy(j).start()

    def relay(j, g):
        h = hops - g
        q_copy(j, h).wait_recv()
        if g == 0:
            rows = dblk(j, at(h), core * tok, tok)
            BIG[rows, :] += PR[j, pl.ds(pr_off[h], tok), :]
        else:
            r_copy(j, g - 1).wait_recv()
            rows = dblk(j, at(h), 0, crows)
            if g == 1:
                BIG[rows, :] += PR[j, pl.ds(pr_off[h], crows), :]
                hrows = dblk(j, at(h), core * tok, tok)
                BIG[hrows, :] += RR[j, pl.ds(rr_off[0], tok), :]
            else:
                BIG[rows, :] += PR[j, pl.ds(pr_off[h], crows), :] + RR[j, pl.ds(rr_off[g - 1], crows), :]
        r_copy(j, g).start()

    def ring(s, static):
        def ok(j):
            return (0 <= j < nj) if static else (j >= 0)
        cond(static, ok(s - hops - 2), lambda: finish(s - hops - 2))
        cond(static, ok(s - hops - 1), lambda: turn(s - hops - 1))
        for g in range(hops - 1, -1, -1):
            cond(static, ok(s - 1 - g), functools.partial(relay, s - 1 - g, g))

    def down_step(j, slot):
        ring(j, False)
        wait(down_copies(j, slot))
        for i in range(n_tiles):
            e = dot(H[pl.ds(i * TILE, TILE), :], V2[slot][TE[i]]).astype(BF16)
            for p in range(3):
                E3[pl.ds(p * slots + i * TILE, TILE), :] = e
        for r in range(group // KC):
            rows = pl.ds(pl.multiple_of(j * group + r * KC, KC), KC)
            BIG[rows, :] = dot(WC[pl.ds(r * KC, KC), :], E3[...])
        for h in range(hops, -1, -1):
            q_copy(j, h).start()

        @pl.when(j + 2 < nj)
        def _():
            start(down_copies(j + 2, slot))

    def down_pair(p, carry):
        for q in range(2):
            down_step(2 * p + q, q)
        return carry

    lax.fori_loop(0, nj // 2, down_pair, 0)
    for s in range(nj, nj + hops + 2):
        ring(s, True)

    def drain(j, carry):
        for h in range(hops):
            r_copy(j, h).wait_send()
        for h in range(hops + 1):
            q_copy(j, h).wait_send()
        f_copy(j).wait_send()
        return carry

    lax.fori_loop(0, nj, drain, 0)


class Dims:
    pass


def solution(mesh):
    n_ep = mesh.shape['ep']
    tok_spec = P(('dp', 'ep'))
    expert_spec = P('ep')

    def device_fn(resid_in, expert_ids, priority, norm_gain, router_w, shared_w1, shared_w3, shared_w2, expert_w1, expert_w3, expert_w2):
        dm = Dims()
        dm.n_chip = n_ep // 2
        dm.tok, dm.hidden = resid_in.shape
        dm.top_k = expert_ids.shape[1]
        dm.local_e = expert_w1.shape[0]
        dm.ff = expert_w1.shape[2]
        dm.capacity = dm.tok * dm.top_k
        dm.nj = dm.hidden // KC
        dm.slots = (dm.capacity + dm.local_e * (TILE - 1)) // TILE * TILE
        hops = dm.n_chip // 2
        assert dm.nj % 2 == 0
        nj, tok, ff, slots = dm.nj, dm.tok, dm.ff, dm.slots
        group = dm.n_chip * 2 * tok

        resid32 = resid_in.astype(F32)
        inv_rms = lax.rsqrt(jnp.mean(resid32 * resid32, axis=1, keepdims=True) + NORM_EPS)
        normed = (resid32 * inv_rms * norm_gain).astype(BF16)
        probs = jax.nn.softmax(jnp.dot(normed, router_w, preferred_element_type=F32), axis=1)
        pick = expert_ids[:, :, None] == jnp.arange(router_w.shape[1], dtype=jnp.int32)
        gates = ROUTE_SCALE * jnp.sum(jnp.where(pick, probs[:, None, :], 0.0), axis=2)
        blocks = normed.reshape(tok, nj, KC).transpose(1, 0, 2)
        shared_act = (jax.nn.silu(dot(normed, shared_w1)) * dot(normed, shared_w3)).astype(BF16)
        shared_out = dot(shared_act, shared_w2).astype(BF16)

        def field(a, fill):
            return jnp.pad(a.astype(F32).T, ((0, KPAD - dm.top_k), (0, 0)), constant_values=fill)

        part = jnp.concatenate([field(expert_ids, -1.0), field(priority, 0.0), field(gates, 0.0)], axis=0)
        core = lax.axis_index('ep') % 2
        info = jnp.concatenate([jnp.where(core == 0, part, 0.0), jnp.where(core == 0, 0.0, part)], axis=1)

        vm = pl.BlockSpec(memory_space=pltpu.VMEM)
        sm = pl.BlockSpec(memory_space=pltpu.SMEM)
        hbm = pl.BlockSpec(memory_space=pl.ANY)
        dma = pltpu.SemaphoreType.DMA
        le = dm.local_e
        rows_all, pick_rows, mix, tile_e = pl.pallas_call(
            functools.partial(gather_kernel, dm),
            out_shape=(jax.ShapeDtypeStruct((nj, dm.n_chip, 2 * tok, KC), BF16), jax.ShapeDtypeStruct((slots, group), BF16),
                       jax.ShapeDtypeStruct((group, 3 * slots), BF16), jax.ShapeDtypeStruct((slots // TILE,), jnp.int32)),
            in_specs=[vm, vm],
            out_specs=(vm, vm, vm, sm),
            scratch_shapes=[
                pltpu.VMEM((dm.n_chip, 2, 3 * KPAD, 2 * tok), F32),
                pltpu.VMEM((dm.n_chip, 2 * tok, KPAD), F32),
                pltpu.VMEM((dm.n_chip, 2 * tok, KPAD), F32),
                dma((2,)),
                dma((hops, nj)), dma((hops, nj)), dma((hops, nj)), dma((hops, nj)),
                dma((hops,)), dma((hops,)), dma((hops,)), dma((hops,)), dma((2,)), dma((2,)),
            ],
            compiler_params=pltpu.CompilerParams(collective_id=0, has_side_effects=True, vmem_limit_bytes=24 << 20),
        )(blocks, info)
        h_act = pl.pallas_call(
            functools.partial(up_kernel, dm),
            out_shape=jax.ShapeDtypeStruct((slots, ff), BF16),
            grid=(nj,),
            in_specs=[sm, pl.BlockSpec((1, dm.n_chip, 2 * tok, KC), lambda j: (j, 0, 0, 0)), vm,
                      pl.BlockSpec((le, KC, ff), lambda j: (0, j, 0)), pl.BlockSpec((le, KC, ff), lambda j: (0, j, 0))],
            out_specs=vm,
            scratch_shapes=[pltpu.VMEM((2 * (ff // KC) * slots, KC), F32)],
            compiler_params=pltpu.CompilerParams(vmem_limit_bytes=40 << 20),
        )(tile_e, rows_all, pick_rows, expert_w1, expert_w3)
        return pl.pallas_call(
            functools.partial(down_kernel, dm),
            out_shape=jax.ShapeDtypeStruct((tok, dm.hidden), BF16),
            in_specs=[vm, vm, sm, vm, vm, hbm],
            out_specs=vm,
            scratch_shapes=[
                pltpu.VMEM((nj * group, KC), F32),
                pltpu.VMEM((le, ff, KC), BF16),
                pltpu.VMEM((le, ff, KC), BF16),
                pltpu.VMEM((3 * slots, KC), BF16),
                pltpu.VMEM((nj, 8 * tok, KC), F32),
                pltpu.VMEM((nj, 7 * tok, KC), F32),
                pltpu.VMEM((nj, tok, KC), F32),
                dma((2,)),
                dma((hops + 1, nj)), dma((hops + 1, nj)), dma((hops, nj)), dma((hops, nj)), dma((nj,)), dma((nj,)),
            ],
            compiler_params=pltpu.CompilerParams(collective_id=1, has_side_effects=True, vmem_limit_bytes=48 << 20),
        )(h_act, mix, tile_e, shared_out, resid_in, expert_w2)

    return jax.shard_map(device_fn, mesh=mesh, in_specs=(tok_spec, tok_spec, tok_spec, P(), P(), P(), P(), P(), expert_spec, expert_spec, expert_spec), out_specs=tok_spec, check_vma=False)
```

time: 361 us -> 203 us (0.56)
  Pallas kernels: 52.6 us -> 171 us
  local copies, waits for them, and re-layouts: 77.4 us -> 2.95 us
  other arithmetic: 70.1 us -> 4.09 us
  waiting for transfers between devices: 65.4 us -> 0 us
  blocking collectives: 54.2 us -> 0 us
  between operations: 13.7 us -> 0.12 us
    pallas_call x0 -> x3, Pallas kernels: none -> 171 us  [the longest x1 76.9 us: device_fn(): pl.pallas_call(functools.partial(down_kernel, dm), out_shape=jax.ShapeDty...]
    reduce_scatter x1 -> x0, waiting for transfers between devices: 65.2 us -> none  [device_fn(): routed = lax.psum_scatter(token_sums, 'ep', scatter_dimension=0, tiled=True)]
    scatter-add x2 -> x0, other arithmetic: 56.1 us -> none  [the longest x1 43.4 us: slot_layout(): jax.ops.segment_sum(mine_kept.astype(jnp.int32), jnp.where(mine_kept, loc...]
    all_gather x3 -> x0, blocking collectives: 54.2 us -> none  [the longest x1 23 us: device_fn(): all_ids = lax.all_gather(expert_ids, 'ep', tiled=True).reshape(-1)]
    gather x9 -> x0, local copies, waits for them, and re-layouts: 52.1 us -> none  [the longest x1 34.3 us: local_keep(): return (mine_int > 0) & (before[prio_flat] < capacity)]
    another operation x3 -> x0, Pallas kernels: 51.2 us -> none
    scatter x1 -> x0, local copies, waits for them, and re-layouts: 23 us -> none  [local_keep(): by_rank = jnp.zeros((n_assign,), jnp.int32).at[prio_flat].set(mine_int)]
    sort x1 -> x0, other arithmetic: 6.73 us -> none  [slot_layout(): slot_order = jnp.argsort(sort_key)[:capacity]]
  transfers between devices with their start and end apart: 2 -> 0, of which waited for: 1 -> 0; matrix products, arithmetic and copies ran while one was open for 36% -> 0% of each run, Pallas kernels for 0% -> 0%
where the time goes in v1:
time: 203 us; the launch traced here: 202 us
  Pallas kernels  171 us (84%)
  matrix products  24 us (12%)
  other arithmetic  4.09 us (2%)
  local copies, waits for them, and re-layouts  2.95 us (1%)
    pallas_call x1, Pallas kernels, device_fn(): pl.pallas_call(functools.partial(down_kernel, dm), out_shape=jax.ShapeDty...  76.9 us
    pallas_call x1, Pallas kernels, device_fn(): pl.pallas_call(functools.partial(gather_kernel, dm), out_shape=(jax.Shape...  63.2 us
    pallas_call x1, Pallas kernels, device_fn(): pl.pallas_call(functools.partial(up_kernel, dm), out_shape=jax.ShapeDtype...  31 us
    dot_general x2, matrix products, dot(): return jnp.dot(a, b, preferred_element_type=F32)  23.8 us

profile of v1, /device:TPU:21, one launch (start us, length us, event | category | flops | bytes accessed | tf_op | source)
XLA Modules:
  0.0 202.3 jit_solution(1995658031834235324)
XLA Ops:
  0.0 0.0 copy-start
  0.0 1.2 fusion.1
  1.2 0.7 convert_bitcast_fusion
  1.9 1.1 fusion.3
  3.0 0.0 copy-done
  3.1 0.2 fusion.9
  3.4 0.1 copy.18
  3.4 0.9 select_reduce_fusion
  4.4 0.1 pad_maximum_fusion.info_ref
  4.5 8.3 %fusion.10 = f32[64,3072]{1,0:T(8,128)S(1)} fusion(bf16[64,2560]{1,0:T(8,128)(2,1)S(1)} %fusion.3, bf16[2560,3072]{1,0:T(8,128)(2,1)} %param.16), kind=kOutput, calls=%fused_computation.31 | convolution fusion | flops 1006632960 | bytes 16842752 | tf_op jit(solution)/shard_map/dot_general | solution.py:20
  12.8 15.5 %convolution_convert_fusion.shared_ref = bf16[64,2560]{1,0:T(8,128)(2,1)S(1)} fusion(bf16[3072,2560]{1,0:T(8,128)(2,1)} %param.18, bf16[64,2560]{1,0:T(8,128)(2,1)S(1)} %fusion.3, bf16[2560,3072]{1,0:T(8,128)(2,1)} %param.17, f32[64,3072]{1,0:T(8,128)S(1)} %fusion.10), kind=kOutput, calls=%fused_computation.1 | convolution fusion | flops 2014609408 | bytes 32899072 | tf_op jit(solution)/shard_map/dot_general | solution.py:20
  28.3 63.2 %shard_map.109 = (bf16[10,8,128,256]{3,2,1,0:T(8,128)(2,1)S(1)}, bf16[768,1024]{1,0:T(8,128)(2,1)S(1)}, bf16[1024,2304]{1,0:T(8,128)(2,1)S(1)}, s32[6]{0:T(128)S(1)}) custom-call(bf16[10,64,256]{2,1,0:T(8,128)(2,1)S(1)} %bitcast.20, f32[24,128]{1,0:T(8,128)S(1)} %pad_maximum_fusion.info_ref), custom_call_target="tpu_custom_call" | custom-call | tf_op jit(solution)/shard_map/pallas_call | solution.py:451
  91.5 0.0 copy-start.2
  91.5 2.1 %copy-done.2 = bf16[1024,2304]{1,0:T(8,128)(2,1)} copy-done((bf16[1024,2304]{1,0:T(8,128)(2,1)}, bf16[1024,2304]{1,0:T(8,128)(2,1)S(1)}, u32[]{:S(2)}) %copy-start.2) | copy-done | bytes 4718616
  93.6 0.0 copy-start.3
  93.7 0.0 copy-start.1
  93.7 31.0 %shard_map.110.H = bf16[768,1536]{1,0:T(8,128)(2,1)S(1)} custom-call(s32[6]{0:T(128)S(1)} %get-tuple-element.9.te_ref.TE, bf16[10,8,128,256]{3,2,1,0:T(8,128)(2,1)S(1)} %get-tuple-element.10.x_ref, bf16[768,1024]{1,0:T(8,128)(2,1)S(1)} %get-tuple-element.11.pg_ref, bf16[4,2560,1536]{2,1,0:T(8,128)(2,1)} %w1_ref.1, bf16[4,2560,1536]{2,1,0:T(8,128)(2,1)} %w3_ref.1), custom_call_target="tpu_custom_call" | custom-call | tf_op jit(solution)/shard_map/pallas_call | solution.py:467
  124.6 0.0 copy-done.3
  124.7 76.9 %shard_map.111 = bf16[64,2560]{1,0:T(8,128)(2,1)S(1)} custom-call(bf16[768,1536]{1,0:T(8,128)(2,1)S(1)} %shard_map.110.H, bf16[1024,2304]{1,0:T(8,128)(2,1)} %copy-done.2, s32[6]{0:T(128)S(1)} %get-tuple-element.9.te_ref.TE, bf16[64,2560]{1,0:T(8,128)(2,1)S(1)} %convolution_convert_fusion.shared_ref, bf16[64,2560]{1,0:T(8,128)(2,1)S(1)} %copy-done.3, ...), custom_call_target="tpu_custom_call" | custom-call | tf_op jit(solution)/shard_map/pallas_call | solution.py:477
  201.5 0.7 copy.23
  202.3 0.0 copy-done.1
  (6 shorter events, 0.1 us)
Async XLA Ops:
  0.0 3.0 %copy-start = (bf16[2560,64]{0,1:T(8,128)(2,1)S(1)}, bf16[2560,64]{0,1:T(8,128)(2,1)}, u32[]{:S(2)}) copy-start(bf16[2560,64]{0,1:T(8,128)(2,1)} %param.15) | copy-start | bytes 983044
  91.5 2.1 %copy-start.2 = (bf16[1024,2304]{1,0:T(8,128)(2,1)}, bf16[1024,2304]{1,0:T(8,128)(2,1)S(1)}, u32[]{:S(2)}) copy-start(bf16[1024,2304]{1,0:T(8,128)(2,1)S(1)} %get-tuple-element.12.WC) | copy-start | bytes 14155780
  93.6 31.0 %copy-start.3 = (bf16[64,2560]{1,0:T(8,128)(2,1)S(1)}, bf16[64,2560]{1,0:T(8,128)(2,1)}, u32[]{:S(2)}) copy-start(bf16[64,2560]{1,0:T(8,128)(2,1)} %resid_ref.1) | copy-start | bytes 983044
  93.7 108.6 %copy-start.1 = (bf16[2560,64]{0,1:T(8,128)(2,1)S(1)}, bf16[2560,64]{0,1:T(8,128)(2,1)}, u32[]{:S(2)}) copy-start(bf16[2560,64]{0,1:T(8,128)(2,1)} %param.15) | copy-start | bytes 983044

commit v2 on v1

--- a/solution.py
+++ b/solution.py
@@ -63,19 +63,40 @@
         c.wait()
 
 
-def gather_kernel(dm, b_ref, info_ref, X, PG, WC, TE,
-                  I, SLT, GLT, lsem, xs_ring, xr_ring, xs_d2d, xr_d2d, is_ring, ir_ring, is_d2d, ir_d2d, p_s, p_r):
+def gather_kernel(dm, b_ref, info_ref, sw1, sw3, X, PG, WC, HS, TE,
+                  I, SLT, GLT, SACC, WS, lsem, wsem, xs_ring, xr_ring, xs_d2d, xr_d2d, is_ring, ir_ring, is_d2d, ir_d2d, p_s, p_r):
     n = dm.n_chip
     hops = n // 2
     tok = dm.tok
     crows = 2 * tok
     nj = dm.nj
-    off = hops + 1
     slots = dm.slots
     n_tiles = slots // TILE
     group = n * crows
     me, chip, core, at, partner, down, up = ring_place(dm)
     half = pl.ds(pl.multiple_of(core * tok, tok), tok)
+    sff = dm.sff
+
+    def shared_copies(t):
+        rows = pl.ds(t * KC, KC)
+        return [pltpu.make_async_copy(src.at[rows, :], WS.at[t % 3, m], wsem.at[t % 3, m]) for m, src in enumerate((sw1, sw3))]
+
+    def shared_stage(t):
+        wait(shared_copies(t))
+        x = b_ref[t]
+        for m in range(2):
+            for c in range(sff // KC):
+                dst = pl.ds(m * sff + c * KC, KC)
+                val = dot(x, WS[t % 3, m, :, pl.ds(c * KC, KC)])
+                if t == 0:
+                    SACC[:, dst] = val
+                else:
+                    SACC[:, dst] += val
+        if t + 3 < nj:
+            start(shared_copies(t + 3))
+
+    for t in range(3):
+        start(shared_copies(t))
     entry_barrier((partner, down, up))
 
     own_x = X.at[:, chip, half, :]
@@ -107,21 +128,13 @@
         blk = X.at[j, at(h), pl.ds(pl.multiple_of((1 - core) * tok, tok), tok), :] if h == hops else X.at[j, at(h)]
         return rcopy(blk, blk, xs_d2d.at[h - 1, j], xr_d2d.at[h - 1, j], partner)
 
-    def comm(s, static):
-        def hop(h):
-            j = s - h
-
-            def run():
-                if h > 0:
-                    x_ring_in(j, h).wait_recv()
-                if h < hops:
-                    x_ring(j, h).start()
-                if h > 0:
-                    x_d2d(j, h).start()
-            cond(static, (j < nj and j >= 0) if static else (j < nj), run)
-        hop(0)
-        for h in range(hops, 0, -1):
-            hop(h)
+    def forward(h, j):
+        if h > 0:
+            x_ring_in(j, h).wait_recv()
+        if h < hops:
+            x_ring(j, h).start()
+        if h > 0:
+            x_d2d(j, h).start()
 
     def i_block(h, rows_half, sign=-1, c=None):
         return I.at[at(sign * h), core if c is None else c] if rows_half else I.at[at(sign * h)]
@@ -137,9 +150,15 @@
             blk = i_block(h, h == hops)
             rcopy(blk, blk, is_d2d.at[h - 1], ir_d2d.at[h - 1], partner).start()
 
-    for s in range(off):
-        comm_info(s)
-        comm(s, True)
+    per = (nj + hops - 1) // hops
+    for h in range(hops):
+        comm_info(h)
+        for j in range(h * per, min((h + 1) * per, nj)):
+            forward(0, j)
+    for j in range(nj // 2 + 1):
+        forward(1, j)
+    comm_info(hops)
+    shared_stage(0)
 
     for h in range(1, hops + 1):
         blk = i_block(h, h == hops, 1, 1 - core)
@@ -211,7 +230,7 @@
     def combine_rows(c):
         sl = SLT[c]
         gl = GLT[c]
-        rows = pl.ds(pl.multiple_of(c * crows, crows), crows)
+        rows = pl.ds(c * crows, crows)
         for p in range(slots // KC):
             scol = (lax.broadcasted_iota(jnp.int32, (crows, KC), 1) + p * KC).astype(F32)
             w = jnp.zeros((crows, KC), F32)
@@ -222,17 +241,23 @@
                 WC[rows, pl.ds(i * slots + p * KC, KC)] = part
                 w = w - part.astype(F32)
 
-    def step(j, carry):
-        comm(j + off, False)
-
-        @pl.when(j < n)
-        def _():
-            combine_rows(j)
-        return carry
-
-    lax.fori_loop(0, nj - 1, step, 0)
-    for c in range(nj - 1, n):
-        combine_rows(c)
+    todo = [(1, j) for j in range(nj // 2 + 1, nj)] + [(h, j) for h in range(2, hops + 1) for j in range(nj)]
+    work = []
+    for t in range(1, nj):
+        work.append(functools.partial(shared_stage, t))
+        if t - 1 < n:
+            work.append(functools.partial(combine_rows, t - 1))
+    last = len(todo) - nj
+    for u, (h, j) in enumerate(todo):
+        forward(h, j)
+        while work and len(work) > (2 * nj - 2) * (last - 1 - u) // last:
+            work.pop(0)()
+    for w in work:
+        w()
+    for c in range(sff // KC):
+        a = SACC[:, pl.ds(c * KC, KC)]
+        g = SACC[:, pl.ds(sff + c * KC, KC)]
+        HS[:, pl.ds(c * KC, KC)] = (jax.nn.silu(a) * g).astype(BF16)
 
     def arrive(j, carry):
         for h in range(1, hops + 1):
@@ -257,33 +282,22 @@
     lax.fori_loop(0, nj, drain, 0)
 
 
-def up_kernel(dm, te_ref, x_ref, pg_ref, w1_ref, w3_ref, h_ref, acc_ref):
-    nt = dm.ff // KC
-    j = pl.program_id(0)
-
-    @pl.when(j == 0)
+def up_kernel(dm, te_ref, x_ref, pg_ref, w1_ref, w3_ref, h_ref, xg_ref):
+    @pl.when(pl.program_id(0) == 0)
     def _():
-        acc_ref[...] = jnp.zeros(acc_ref.shape, F32)
-
-    xg = dot(pg_ref[...], x_ref[0].reshape(pg_ref.shape[1], KC)).astype(BF16)
+        for j in range(dm.nj):
+            xg_ref[:, pl.ds(j * KC, KC)] = dot(pg_ref[...], x_ref[j].reshape(pg_ref.shape[1], KC)).astype(BF16)
+
     for i in range(dm.slots // TILE):
-        xi = xg[i * TILE:(i + 1) * TILE]
-        for m, w_ref in enumerate((w1_ref, w3_ref)):
-            for c in range(nt):
-                rows = pl.ds((m * nt + c) * dm.slots + i * TILE, TILE)
-                acc_ref[rows, :] += dot(xi, w_ref[te_ref[i], :, pl.ds(c * KC, KC)])
-
-    @pl.when(j == pl.num_programs(0) - 1)
-    def _():
-        for i in range(dm.slots // TILE):
-            for c in range(nt):
-                a = acc_ref[pl.ds(c * dm.slots + i * TILE, TILE), :]
-                g = acc_ref[pl.ds((nt + c) * dm.slots + i * TILE, TILE), :]
-                h_ref[pl.ds(i * TILE, TILE), pl.ds(c * KC, KC)] = (jax.nn.silu(a) * g).astype(BF16)
-
-
-def down_kernel(dm, H, WC, TE, shared_ref, resid_ref, ew2, out_ref,
-                BIG, V2A, V2B, E3, PR, RR, FR, vsem, qs, qr, rs, rr, fs, fr):
+        rows = pl.ds(i * TILE, TILE)
+        e = te_ref[i]
+        a = dot(xg_ref[rows, :], w1_ref[e])
+        g = dot(xg_ref[rows, :], w3_ref[e])
+        h_ref[rows, :] = (jax.nn.silu(a) * g).astype(BF16)
+
+
+def down_kernel(dm, H, WC, TE, HS, resid_ref, ew2, sw2, out_ref,
+                BIG, V2A, V2B, S2A, S2B, E3, PR, RR, FR, SOUT, vsem, qs, qr, rs, rr, fs, fr):
     n = dm.n_chip
     hops = n // 2
     tok = dm.tok
@@ -294,10 +308,12 @@
     group = n * crows
     me, chip, core, at, partner, down, up = ring_place(dm)
     V2 = (V2A, V2B)
+    S2 = (S2A, S2B)
 
     def down_copies(j, slot):
         cols = pl.ds(pl.multiple_of(j * KC, KC), KC)
-        return [pltpu.make_async_copy(ew2.at[:, :, cols], V2[slot], vsem.at[slot])]
+        return [pltpu.make_async_copy(ew2.at[:, :, cols], V2[slot], vsem.at[slot, 0]),
+                pltpu.make_async_copy(sw2.at[:, cols], S2[slot], vsem.at[slot, 1])]
 
     start(down_copies(0, 0))
     start(down_copies(1, 1))
@@ -334,7 +350,7 @@
         cols = pl.ds(pl.multiple_of(j * KC, KC), KC)
         routed = BIG[dblk(j, chip, core * tok, tok), :] + PR[j, pl.ds(pr_off[0], tok), :]
         routed = routed + RR[j, pl.ds(pl.multiple_of(rr_off[hops - 1] + core * tok, tok), tok), :] + FR[j]
-        out_ref[:, cols] = (resid_ref[:, cols].astype(F32) + shared_ref[:, cols].astype(F32) + routed).astype(BF16)
+        out_ref[:, cols] = (resid_ref[:, cols].astype(F32) + SOUT[j].astype(F32) + routed).astype(BF16)
 
     def turn(j):
         r_copy(j, hops - 1).wait_recv()
@@ -360,10 +376,10 @@
     def ring(s, static):
         def ok(j):
             return (0 <= j < nj) if static else (j >= 0)
+        for g in range(hops):
+            cond(static, ok(s - 1 - g), functools.partial(relay, s - 1 - g, g))
+        cond(static, ok(s - hops - 1), lambda: turn(s - hops - 1))
         cond(static, ok(s - hops - 2), lambda: finish(s - hops - 2))
-        cond(static, ok(s - hops - 1), lambda: turn(s - hops - 1))
-        for g in range(hops - 1, -1, -1):
-            cond(static, ok(s - 1 - g), functools.partial(relay, s - 1 - g, g))
 
     def down_step(j, slot):
         ring(j, False)
@@ -375,6 +391,7 @@
         for r in range(group // KC):
             rows = pl.ds(pl.multiple_of(j * group + r * KC, KC), KC)
             BIG[rows, :] = dot(WC[pl.ds(r * KC, KC), :], E3[...])
+        SOUT[j] = dot(HS[...], S2[slot][...]).astype(BF16)
         for h in range(hops, -1, -1):
             q_copy(j, h).start()
 
@@ -420,6 +437,7 @@
         dm.ff = expert_w1.shape[2]
         dm.capacity = dm.tok * dm.top_k
         dm.nj = dm.hidden // KC
+        dm.sff = shared_w1.shape[1]
         dm.slots = (dm.capacity + dm.local_e * (TILE - 1)) // TILE * TILE
         hops = dm.n_chip // 2
         assert dm.nj % 2 == 0
@@ -433,8 +451,6 @@
         pick = expert_ids[:, :, None] == jnp.arange(router_w.shape[1], dtype=jnp.int32)
         gates = ROUTE_SCALE * jnp.sum(jnp.where(pick, probs[:, None, :], 0.0), axis=2)
         blocks = normed.reshape(tok, nj, KC).transpose(1, 0, 2)
-        shared_act = (jax.nn.silu(dot(normed, shared_w1)) * dot(normed, shared_w3)).astype(BF16)
-        shared_out = dot(shared_act, shared_w2).astype(BF16)
 
         def field(a, fill):
             return jnp.pad(a.astype(F32).T, ((0, KPAD - dm.top_k), (0, 0)), constant_values=fill)
@@ -448,49 +464,55 @@
         hbm = pl.BlockSpec(memory_space=pl.ANY)
         dma = pltpu.SemaphoreType.DMA
         le = dm.local_e
-        rows_all, pick_rows, mix, tile_e = pl.pallas_call(
+        rows_all, pick_rows, mix, shared_act, tile_e = pl.pallas_call(
             functools.partial(gather_kernel, dm),
             out_shape=(jax.ShapeDtypeStruct((nj, dm.n_chip, 2 * tok, KC), BF16), jax.ShapeDtypeStruct((slots, group), BF16),
-                       jax.ShapeDtypeStruct((group, 3 * slots), BF16), jax.ShapeDtypeStruct((slots // TILE,), jnp.int32)),
-            in_specs=[vm, vm],
-            out_specs=(vm, vm, vm, sm),
+                       jax.ShapeDtypeStruct((group, 3 * slots), BF16), jax.ShapeDtypeStruct((tok, dm.sff), BF16),
+                       jax.ShapeDtypeStruct((slots // TILE,), jnp.int32)),
+            in_specs=[vm, vm, hbm, hbm],
+            out_specs=(vm, vm, vm, vm, sm),
             scratch_shapes=[
                 pltpu.VMEM((dm.n_chip, 2, 3 * KPAD, 2 * tok), F32),
                 pltpu.VMEM((dm.n_chip, 2 * tok, KPAD), F32),
                 pltpu.VMEM((dm.n_chip, 2 * tok, KPAD), F32),
-                dma((2,)),
+                pltpu.VMEM((tok, 2 * dm.sff), F32),
+                pltpu.VMEM((3, 2, KC, dm.sff), BF16),
+                dma((2,)), dma((3, 2)),
                 dma((hops, nj)), dma((hops, nj)), dma((hops, nj)), dma((hops, nj)),
                 dma((hops,)), dma((hops,)), dma((hops,)), dma((hops,)), dma((2,)), dma((2,)),
             ],
-            compiler_params=pltpu.CompilerParams(collective_id=0, has_side_effects=True, vmem_limit_bytes=24 << 20),
-        )(blocks, info)
+            compiler_params=pltpu.CompilerParams(collective_id=0, has_side_effects=True, vmem_limit_bytes=22 << 20),
+        )(blocks, info, shared_w1, shared_w3)
         h_act = pl.pallas_call(
             functools.partial(up_kernel, dm),
             out_shape=jax.ShapeDtypeStruct((slots, ff), BF16),
-            grid=(nj,),
-            in_specs=[sm, pl.BlockSpec((1, dm.n_chip, 2 * tok, KC), lambda j: (j, 0, 0, 0)), vm,
-                      pl.BlockSpec((le, KC, ff), lambda j: (0, j, 0)), pl.BlockSpec((le, KC, ff), lambda j: (0, j, 0))],
-            out_specs=vm,
-            scratch_shapes=[pltpu.VMEM((2 * (ff // KC) * slots, KC), F32)],
-            compiler_params=pltpu.CompilerParams(vmem_limit_bytes=40 << 20),
+            grid=(ff // KC,),
+            in_specs=[sm, vm, vm,
+                      pl.BlockSpec((le, dm.hidden, KC), lambda c: (0, 0, c)), pl.BlockSpec((le, dm.hidden, KC), lambda c: (0, 0, c))],
+            out_specs=pl.BlockSpec((slots, KC), lambda c: (0, c)),
+            scratch_shapes=[pltpu.VMEM((slots, dm.hidden), BF16)],
+            compiler_params=pltpu.CompilerParams(vmem_limit_bytes=30 << 20),
         )(tile_e, rows_all, pick_rows, expert_w1, expert_w3)
         return pl.pallas_call(
             functools.partial(down_kernel, dm),
             out_shape=jax.ShapeDtypeStruct((tok, dm.hidden), BF16),
-            in_specs=[vm, vm, sm, vm, vm, hbm],
+            in_specs=[vm, vm, sm, vm, vm, hbm, hbm],
             out_specs=vm,
             scratch_shapes=[
                 pltpu.VMEM((nj * group, KC), F32),
                 pltpu.VMEM((le, ff, KC), BF16),
                 pltpu.VMEM((le, ff, KC), BF16),
+                pltpu.VMEM((dm.sff, KC), BF16),
+                pltpu.VMEM((dm.sff, KC), BF16),
                 pltpu.VMEM((3 * slots, KC), BF16),
                 pltpu.VMEM((nj, 8 * tok, KC), F32),
                 pltpu.VMEM((nj, 7 * tok, KC), F32),
                 pltpu.VMEM((nj, tok, KC), F32),
-                dma((2,)),
+                pltpu.VMEM((nj, tok, KC), BF16),
+                dma((2, 2)),
                 dma((hops + 1, nj)), dma((hops + 1, nj)), dma((hops, nj)), dma((hops, nj)), dma((nj,)), dma((nj,)),
             ],
-            compiler_params=pltpu.CompilerParams(collective_id=1, has_side_effects=True, vmem_limit_bytes=48 << 20),
-        )(h_act, mix, tile_e, shared_out, resid_in, expert_w2)
+            compiler_params=pltpu.CompilerParams(collective_id=1, has_side_effects=True, vmem_limit_bytes=38 << 20),
+        )(h_act, mix, tile_e, shared_act, resid_in, expert_w2, shared_w2)
 
     return jax.shard_map(device_fn, mesh=mesh, in_specs=(tok_spec, tok_spec, tok_spec, P(), P(), P(), P(), P(), expert_spec, expert_spec, expert_spec), out_specs=tok_spec, check_vma=False)

time: 203 us -> 154 us (0.76)
  Pallas kernels: 171 us -> 143 us
  matrix products: 24 us -> 0.25 us
  local copies, waits for them, and re-layouts: 2.95 us -> 6.31 us
    dot_general x2 -> x0, matrix products: 23.8 us -> none  [dot(): return jnp.dot(a, b, preferred_element_type=F32)]
    pallas_call x1, Pallas kernels: 63.2 us -> 45.1 us  [device_fn(): pl.pallas_call(functools.partial(gather_kernel, dm), out_shape=(jax.Shape...]
    pallas_call x1, Pallas kernels: 76.9 us -> 71.2 us  [device_fn(): pl.pallas_call(functools.partial(down_kernel, dm), out_shape=jax.ShapeDty...]
    pallas_call x1, Pallas kernels: 31 us -> 26.9 us  [device_fn(): pl.pallas_call(functools.partial(up_kernel, dm), out_shape=jax.ShapeDtype...]
    unnamed x9, local copies, waits for them, and re-layouts: 2.86 us -> 6.21 us
where the time goes in v2:
time: 154 us
  Pallas kernels  143 us (93%)
  local copies, waits for them, and re-layouts  6.31 us (4%)
  other arithmetic  4.09 us (3%)
    pallas_call x1, Pallas kernels, device_fn(): pl.pallas_call(functools.partial(down_kernel, dm), out_shape=jax.ShapeDty...  71.2 us
    pallas_call x1, Pallas kernels, device_fn(): pl.pallas_call(functools.partial(gather_kernel, dm), out_shape=(jax.Shape...  45.1 us
    pallas_call x1, Pallas kernels, device_fn(): pl.pallas_call(functools.partial(up_kernel, dm), out_shape=jax.ShapeDtype...  26.9 us
    unnamed x9, local copies, waits for them, and re-layouts  6.21 us

profile of v2, /device:TPU:21, one launch (start us, length us, event | category | flops | bytes accessed | tf_op | source)
XLA Modules:
  0.0 154.0 jit_solution(29040691002076274)
XLA Ops:
  0.0 0.0 copy-start
  0.0 1.2 fusion
  1.2 0.7 convert_bitcast_fusion
  1.9 1.1 fusion.2
  3.0 0.0 copy-done
  3.1 0.2 fusion.6
  3.4 0.1 copy.18
  3.4 0.9 select_reduce_fusion
  4.4 0.1 pad_maximum_fusion.info_ref
  4.5 0.0 copy-start.2
  4.5 5.5 %copy-done.2 = bf16[2560,3072]{1,0:T(8,128)(2,1)S(1)} copy-done((bf16[2560,3072]{1,0:T(8,128)(2,1)S(1)}, bf16[2560,3072]{1,0:T(8,128)(2,1)}, u32[]{:S(2)}) %copy-start.2) | copy-done | bytes 15728664
  10.0 45.1 %shard_map.109 = (bf16[10,8,128,256]{3,2,1,0:T(8,128)(2,1)S(1)}, bf16[768,1024]{1,0:T(8,128)(2,1)S(1)}, bf16[1024,2304]{1,0:T(8,128)(2,1)S(1)}, bf16[64,3072]{1,0:T(8,128)(2,1)S(1)}, s32[6]{0:T(128)S(1)}) custom-call(bf16[10,64,256]{2,1,0:T(8,128)(2,1)S(1)} %bitcast.15, f32[24,128]{1,0:T(8,128)S(1)} %pad_maximum_fusion.info_ref, ...), custom_call_target="tpu_custom_call" | custom-call | tf_op jit(solution)/shard_map/pallas_call | solution.py:467
  55.1 0.0 copy-start.3
  55.1 0.0 copy-start.1
  55.1 26.9 %shard_map.110.H = bf16[768,1536]{1,0:T(8,128)(2,1)S(1)} custom-call(s32[6]{0:T(128)S(1)} %get-tuple-element.10.te_ref.TE, bf16[10,8,128,256]{3,2,1,0:T(8,128)(2,1)S(1)} %get-tuple-element.11.x_ref, bf16[768,1024]{1,0:T(8,128)(2,1)S(1)} %get-tuple-element.12.pg_ref, bf16[4,2560,1536]{2,1,0:T(8,128)(2,1)} %w1_ref.1, bf16[4,2560,1536]{2,1,0:T(8,128)(2,1)} %w3_ref.1), custom_call_target="tpu_custom_call" | custom-call | tf_op jit(solution)/shard_map/pallas_call | solution.py:486
  82.0 0.0 copy-done.3
  82.0 71.2 %shard_map.111 = bf16[64,2560]{1,0:T(8,128)(2,1)S(1)} custom-call(bf16[768,1536]{1,0:T(8,128)(2,1)S(1)} %shard_map.110.H, bf16[1024,2304]{1,0:T(8,128)(2,1)S(1)} %get-tuple-element.13.WC, s32[6]{0:T(128)S(1)} %get-tuple-element.10.te_ref.TE, bf16[64,3072]{1,0:T(8,128)(2,1)S(1)} %get-tuple-element.14.HS, bf16[64,2560]{1,0:T(8,128)(2,1)S(1)} %copy-done.3, ...), custom_call_target="tpu_custom_call" | custom-call | tf_op jit(solution)/shard_map/pallas_call | solution.py:496
  153.2 0.7 copy.23
  154.0 0.0 copy-done.1
  (6 shorter events, 0.1 us)
Async XLA Ops:
  0.0 3.0 %copy-start = (bf16[2560,64]{0,1:T(8,128)(2,1)S(1)}, bf16[2560,64]{0,1:T(8,128)(2,1)}, u32[]{:S(2)}) copy-start(bf16[2560,64]{0,1:T(8,128)(2,1)} %param.15) | copy-start | bytes 983044
  4.5 5.5 %copy-start.2 = (bf16[2560,3072]{1,0:T(8,128)(2,1)S(1)}, bf16[2560,3072]{1,0:T(8,128)(2,1)}, u32[]{:S(2)}) copy-start(bf16[2560,3072]{1,0:T(8,128)(2,1)} %sw1.1) | copy-start | bytes 47185924
  55.1 26.9 %copy-start.3 = (bf16[64,2560]{1,0:T(8,128)(2,1)S(1)}, bf16[64,2560]{1,0:T(8,128)(2,1)}, u32[]{:S(2)}) copy-start(bf16[64,2560]{1,0:T(8,128)(2,1)} %resid_ref.1) | copy-start | bytes 983044
  55.1 98.9 %copy-start.1 = (bf16[2560,64]{0,1:T(8,128)(2,1)S(1)}, bf16[2560,64]{0,1:T(8,128)(2,1)}, u32[]{:S(2)}) copy-start(bf16[2560,64]{0,1:T(8,128)(2,1)} %param.15) | copy-start | bytes 983044

commit v3 on v2

--- a/solution.py
+++ b/solution.py
@@ -63,8 +63,8 @@
         c.wait()
 
 
-def gather_kernel(dm, b_ref, info_ref, sw1, sw3, X, PG, WC, HS, TE,
-                  I, SLT, GLT, SACC, WS, lsem, wsem, xs_ring, xr_ring, xs_d2d, xr_d2d, is_ring, ir_ring, is_d2d, ir_d2d, p_s, p_r):
+def gather_kernel(dm, b_ref, info_ref, sw1, sw3, XG, WC, HS, TE,
+                  X, PG, I, SLT, GLT, SACC, WS, lsem, wsem, xs_ring, xr_ring, xs_d2d, xr_d2d, is_ring, ir_ring, is_d2d, ir_d2d, p_s, p_r):
     n = dm.n_chip
     hops = n // 2
     tok = dm.tok
@@ -79,7 +79,7 @@
 
     def shared_copies(t):
         rows = pl.ds(t * KC, KC)
-        return [pltpu.make_async_copy(src.at[rows, :], WS.at[t % 3, m], wsem.at[t % 3, m]) for m, src in enumerate((sw1, sw3))]
+        return [pltpu.make_async_copy(src.at[rows, :], WS.at[t % 2, m], wsem.at[t % 2, m]) for m, src in enumerate((sw1, sw3))]
 
     def shared_stage(t):
         wait(shared_copies(t))
@@ -87,15 +87,15 @@
         for m in range(2):
             for c in range(sff // KC):
                 dst = pl.ds(m * sff + c * KC, KC)
-                val = dot(x, WS[t % 3, m, :, pl.ds(c * KC, KC)])
+                val = dot(x, WS[t % 2, m, :, pl.ds(c * KC, KC)])
                 if t == 0:
                     SACC[:, dst] = val
                 else:
                     SACC[:, dst] += val
-        if t + 3 < nj:
-            start(shared_copies(t + 3))
-
-    for t in range(3):
+        if t + 2 < nj:
+            start(shared_copies(t + 2))
+
+    for t in range(2):
         start(shared_copies(t))
     entry_barrier((partner, down, up))
 
@@ -150,15 +150,26 @@
             blk = i_block(h, h == hops)
             rcopy(blk, blk, is_d2d.at[h - 1], ir_d2d.at[h - 1], partner).start()
 
-    per = (nj + hops - 1) // hops
-    for h in range(hops):
-        comm_info(h)
-        for j in range(h * per, min((h + 1) * per, nj)):
-            forward(0, j)
-    for j in range(nj // 2 + 1):
+    comm_info(0)
+    for j in range(nj // 2):
+        forward(0, j)
+    comm_info(1)
+    for j in range(nj // 2, nj):
+        forward(0, j)
+    for j in range(3):
         forward(1, j)
+    shared_stage(0)
+    comm_info(2)
+    for j in range(3, 7):
+        forward(1, j)
+    shared_stage(1)
+    for j in range(7, nj):
+        forward(1, j)
+    comm_info(3)
+    shared_stage(2)
+    for j in range(4):
+        forward(2, j)
     comm_info(hops)
-    shared_stage(0)
 
     for h in range(1, hops + 1):
         blk = i_block(h, h == hops, 1, 1 - core)
@@ -226,6 +237,7 @@
 
     for i in range(n_tiles):
         TE[i] = tile_e[i]
+    TE[n_tiles] = bounds[dm.local_e - 1]
 
     def combine_rows(c):
         sl = SLT[c]
@@ -241,30 +253,45 @@
                 WC[rows, pl.ds(i * slots + p * KC, KC)] = part
                 w = w - part.astype(F32)
 
-    todo = [(1, j) for j in range(nj // 2 + 1, nj)] + [(h, j) for h in range(2, hops + 1) for j in range(nj)]
+    todo = [(2, j) for j in range(4, nj)] + [(3, j) for j in range(nj)]
     work = []
-    for t in range(1, nj):
-        work.append(functools.partial(shared_stage, t))
-        if t - 1 < n:
-            work.append(functools.partial(combine_rows, t - 1))
-    last = len(todo) - nj
+    for t in range(max(nj - 3, n)):
+        if t < n:
+            work.append(functools.partial(combine_rows, t))
+        if t < nj - 3:
+            work.append(functools.partial(shared_stage, t + 3))
+    total = len(work)
     for u, (h, j) in enumerate(todo):
         forward(h, j)
-        while work and len(work) > (2 * nj - 2) * (last - 1 - u) // last:
+        while len(work) > total * (len(todo) - 1 - u) // len(todo):
             work.pop(0)()
-    for w in work:
-        w()
     for c in range(sff // KC):
         a = SACC[:, pl.ds(c * KC, KC)]
         g = SACC[:, pl.ds(sff + c * KC, KC)]
         HS[:, pl.ds(c * KC, KC)] = (jax.nn.silu(a) * g).astype(BF16)
 
-    def arrive(j, carry):
+    def pick(j):
         for h in range(1, hops + 1):
             x_d2d_in(j, h).wait_recv()
+        XG[:, pl.ds(pl.multiple_of(j * KC, KC), KC)] = dot(PG[...], X[j].reshape(group, KC)).astype(BF16)
+
+    lag = 3
+    for j in range(lag):
+        forward(hops, j)
+
+    def last_hop(j, carry):
+        forward(hops, j)
+        pick(j - lag)
         return carry
 
-    lax.fori_loop(0, nj, arrive, 0)
+    lax.fori_loop(lag, nj, last_hop, 0)
+
+    def last_pick(j, carry):
+        pick(j)
+        return carry
+
+    lax.fori_loop(nj - lag, nj, last_pick, 0)
+
     for c in first:
         c.wait_send()
     for h in range(hops):
@@ -282,18 +309,21 @@
     lax.fori_loop(0, nj, drain, 0)
 
 
-def up_kernel(dm, te_ref, x_ref, pg_ref, w1_ref, w3_ref, h_ref, xg_ref):
-    @pl.when(pl.program_id(0) == 0)
-    def _():
-        for j in range(dm.nj):
-            xg_ref[:, pl.ds(j * KC, KC)] = dot(pg_ref[...], x_ref[j].reshape(pg_ref.shape[1], KC)).astype(BF16)
-
-    for i in range(dm.slots // TILE):
+def up_kernel(dm, te_ref, xg_ref, w1_ref, w3_ref, h_ref):
+    n_tiles = dm.slots // TILE
+    for i in range(n_tiles):
         rows = pl.ds(i * TILE, TILE)
-        e = te_ref[i]
-        a = dot(xg_ref[rows, :], w1_ref[e])
-        g = dot(xg_ref[rows, :], w3_ref[e])
-        h_ref[rows, :] = (jax.nn.silu(a) * g).astype(BF16)
+
+        @pl.when(i < te_ref[n_tiles])
+        def _():
+            e = te_ref[i]
+            a = dot(xg_ref[rows, :], w1_ref[e])
+            g = dot(xg_ref[rows, :], w3_ref[e])
+            h_ref[rows, :] = (jax.nn.silu(a) * g).astype(BF16)
+
+        @pl.when(i >= te_ref[n_tiles])
+        def _():
+            h_ref[rows, :] = jnp.zeros((TILE, KC), BF16)
 
 
 def down_kernel(dm, H, WC, TE, HS, resid_ref, ew2, sw2, out_ref,
@@ -373,13 +403,16 @@
                 BIG[rows, :] += PR[j, pl.ds(pr_off[h], crows), :] + RR[j, pl.ds(rr_off[g - 1], crows), :]
         r_copy(j, g).start()
 
+    skew = 2
+
     def ring(s, static):
         def ok(j):
             return (0 <= j < nj) if static else (j >= 0)
-        for g in range(hops):
-            cond(static, ok(s - 1 - g), functools.partial(relay, s - 1 - g, g))
-        cond(static, ok(s - hops - 1), lambda: turn(s - hops - 1))
-        cond(static, ok(s - hops - 2), lambda: finish(s - hops - 2))
+        for g in range(1, hops):
+            cond(static, ok(s - 1 - skew * g), functools.partial(relay, s - 1 - skew * g, g))
+        cond(static, ok(s - 1), functools.partial(relay, s - 1, 0))
+        cond(static, ok(s - 1 - skew * hops), lambda: turn(s - 1 - skew * hops))
+        cond(static, ok(s - 2 - skew * hops), lambda: finish(s - 2 - skew * hops))
 
     def down_step(j, slot):
         ring(j, False)
@@ -391,9 +424,9 @@
         for r in range(group // KC):
             rows = pl.ds(pl.multiple_of(j * group + r * KC, KC), KC)
             BIG[rows, :] = dot(WC[pl.ds(r * KC, KC), :], E3[...])
-        SOUT[j] = dot(HS[...], S2[slot][...]).astype(BF16)
         for h in range(hops, -1, -1):
             q_copy(j, h).start()
+        SOUT[j] = dot(HS[...], S2[slot][...]).astype(BF16)
 
         @pl.when(j + 2 < nj)
         def _():
@@ -405,7 +438,7 @@
         return carry
 
     lax.fori_loop(0, nj // 2, down_pair, 0)
-    for s in range(nj, nj + hops + 2):
+    for s in range(nj, nj + skew * hops + 2):
         ring(s, True)
 
     def drain(j, carry):
@@ -461,38 +494,41 @@
 
         vm = pl.BlockSpec(memory_space=pltpu.VMEM)
         sm = pl.BlockSpec(memory_space=pltpu.SMEM)
-        hbm = pl.BlockSpec(memory_space=pl.ANY)
+        hbm = pl.BlockSpec(memory_space=pltpu.HBM)
         dma = pltpu.SemaphoreType.DMA
         le = dm.local_e
-        rows_all, pick_rows, mix, shared_act, tile_e = pl.pallas_call(
+        picked, mix, shared_act, tile_e = pl.pallas_call(
             functools.partial(gather_kernel, dm),
-            out_shape=(jax.ShapeDtypeStruct((nj, dm.n_chip, 2 * tok, KC), BF16), jax.ShapeDtypeStruct((slots, group), BF16),
+            out_shape=(jax.ShapeDtypeStruct((slots, dm.hidden), BF16),
                        jax.ShapeDtypeStruct((group, 3 * slots), BF16), jax.ShapeDtypeStruct((tok, dm.sff), BF16),
-                       jax.ShapeDtypeStruct((slots // TILE,), jnp.int32)),
+                       jax.ShapeDtypeStruct((slots // TILE + 1,), jnp.int32)),
             in_specs=[vm, vm, hbm, hbm],
-            out_specs=(vm, vm, vm, vm, sm),
+            out_specs=(vm, vm, vm, sm),
             scratch_shapes=[
+                pltpu.VMEM((nj, dm.n_chip, 2 * tok, KC), BF16),
+                pltpu.VMEM((slots, group), BF16),
                 pltpu.VMEM((dm.n_chip, 2, 3 * KPAD, 2 * tok), F32),
                 pltpu.VMEM((dm.n_chip, 2 * tok, KPAD), F32),
                 pltpu.VMEM((dm.n_chip, 2 * tok, KPAD), F32),
                 pltpu.VMEM((tok, 2 * dm.sff), F32),
-                pltpu.VMEM((3, 2, KC, dm.sff), BF16),
-                dma((2,)), dma((3, 2)),
+                pltpu.VMEM((2, 2, KC, dm.sff), BF16),
+                dma((2,)), dma((2, 2)),
                 dma((hops, nj)), dma((hops, nj)), dma((hops, nj)), dma((hops, nj)),
                 dma((hops,)), dma((hops,)), dma((hops,)), dma((hops,)), dma((2,)), dma((2,)),
             ],
-            compiler_params=pltpu.CompilerParams(collective_id=0, has_side_effects=True, vmem_limit_bytes=22 << 20),
+            compiler_params=pltpu.CompilerParams(collective_id=0, has_side_effects=True, vmem_limit_bytes=46 << 20),
+            cost_estimate=pl.CostEstimate(flops=35_000_000_000, bytes_accessed=40_000_000, transcendentals=0),
         )(blocks, info, shared_w1, shared_w3)
         h_act = pl.pallas_call(
             functools.partial(up_kernel, dm),
             out_shape=jax.ShapeDtypeStruct((slots, ff), BF16),
             grid=(ff // KC,),
-            in_specs=[sm, vm, vm,
+            in_specs=[sm, vm,
                       pl.BlockSpec((le, dm.hidden, KC), lambda c: (0, 0, c)), pl.BlockSpec((le, dm.hidden, KC), lambda c: (0, 0, c))],
             out_specs=pl.BlockSpec((slots, KC), lambda c: (0, c)),
-            scratch_shapes=[pltpu.VMEM((slots, dm.hidden), BF16)],
-            compiler_params=pltpu.CompilerParams(vmem_limit_bytes=30 << 20),
-        )(tile_e, rows_all, pick_rows, expert_w1, expert_w3)
+            compiler_params=pltpu.CompilerParams(vmem_limit_bytes=44 << 20),
+            cost_estimate=pl.CostEstimate(flops=10_000_000_000, bytes_accessed=70_000_000, transcendentals=0),
+        )(tile_e, picked, expert_w1, expert_w3)
         return pl.pallas_call(
             functools.partial(down_kernel, dm),
             out_shape=jax.ShapeDtypeStruct((tok, dm.hidden), BF16),

time: 154 us -> 149 us (0.968)
  local copies, waits for them, and re-layouts: 6.31 us -> 0.84 us
    pallas_call x1, Pallas kernels: 45.1 us -> 50.6 us  [device_fn(): pl.pallas_call(functools.partial(gather_kernel, dm), out_shape=(jax.Shape...]
    unnamed x9, local copies, waits for them, and re-layouts: 6.21 us -> 0.75 us
    pallas_call x1, Pallas kernels: 26.9 us -> 23.5 us  [device_fn(): pl.pallas_call(functools.partial(up_kernel, dm), out_shape=jax.ShapeDtype...]
    pallas_call x1, Pallas kernels: 71.2 us -> 69.7 us  [device_fn(): pl.pallas_call(functools.partial(down_kernel, dm), out_shape=jax.ShapeDty...]
where the time goes in v3:
time: 149 us
  Pallas kernels  144 us (97%)
  other arithmetic  4.09 us (3%)
    pallas_call x1, Pallas kernels, device_fn(): pl.pallas_call(functools.partial(down_kernel, dm), out_shape=jax.ShapeDty...  69.7 us
    pallas_call x1, Pallas kernels, device_fn(): pl.pallas_call(functools.partial(gather_kernel, dm), out_shape=(jax.Shape...  50.6 us
    pallas_call x1, Pallas kernels, device_fn(): pl.pallas_call(functools.partial(up_kernel, dm), out_shape=jax.ShapeDtype...  23.5 us

profile of v3, /device:TPU:21, one launch (start us, length us, event | category | flops | bytes accessed | tf_op | source)
XLA Modules:
  0.0 149.1 jit_solution(11062556971272593436)
XLA Ops:
  0.0 0.0 copy-start
  0.0 1.2 fusion
  1.2 0.7 convert_bitcast_fusion
  1.9 1.1 fusion.2
  3.0 0.0 copy-done
  3.1 0.2 fusion.6
  3.4 0.1 copy.18
  3.4 0.9 select_reduce_fusion
  4.4 0.1 pad_maximum_fusion.info_ref
  4.5 50.6 %shard_map.109 = (bf16[768,2560]{1,0:T(8,128)(2,1)S(1)}, bf16[1024,2304]{1,0:T(8,128)(2,1)}, bf16[64,3072]{1,0:T(8,128)(2,1)S(1)}, s32[7]{0:T(128)S(1)}) custom-call(bf16[10,64,256]{2,1,0:T(8,128)(2,1)S(1)} %bitcast.15, f32[24,128]{1,0:T(8,128)S(1)} %pad_maximum_fusion.info_ref, bf16[2560,3072]{1,0:T(8,128)(2,1)} %sw1.1, bf16[2560,3072]{1,0:T(8,128)(2,1)} %sw3.1), custom_call_target="tpu_custom_call" | custom-call | flops 35000000512 | bytes 40000000 | tf_op jit(solution)/shard_map/pallas_call | solution.py:500
  55.1 0.0 copy-start.2
  55.1 0.0 copy-start.3
  55.1 0.0 copy-start.1
  55.2 23.5 %shard_map.110.H = bf16[768,1536]{1,0:T(8,128)(2,1)S(1)} custom-call(s32[7]{0:T(128)S(1)} %get-tuple-element.9.te_ref.TE, bf16[768,2560]{1,0:T(8,128)(2,1)S(1)} %get-tuple-element.10.xg_ref, bf16[4,2560,1536]{2,1,0:T(8,128)(2,1)} %w1_ref.1, bf16[4,2560,1536]{2,1,0:T(8,128)(2,1)} %w3_ref.1), custom_call_target="tpu_custom_call" | custom-call | flops 10000000000 | bytes 70000000 | tf_op jit(solution)/shard_map/pallas_call | solution.py:522
  78.7 0.0 copy-done.2
  78.7 0.0 copy-done.3
  78.7 69.7 %shard_map.111 = bf16[64,2560]{1,0:T(8,128)(2,1)S(1)} custom-call(bf16[768,1536]{1,0:T(8,128)(2,1)S(1)} %shard_map.110.H, bf16[1024,2304]{1,0:T(8,128)(2,1)S(1)} %copy-done.2, s32[7]{0:T(128)S(1)} %get-tuple-element.9.te_ref.TE, bf16[64,3072]{1,0:T(8,128)(2,1)S(1)} %get-tuple-element.12.HS, bf16[64,2560]{1,0:T(8,128)(2,1)S(1)} %copy-done.3, ...), custom_call_target="tpu_custom_call" | custom-call | tf_op jit(solution)/shard_map/pallas_call | solution.py:532
  148.4 0.7 copy.23
  149.1 0.0 copy-done.1
  (6 shorter events, 0.1 us)
Async XLA Ops:
  0.0 3.0 %copy-start = (bf16[2560,64]{0,1:T(8,128)(2,1)S(1)}, bf16[2560,64]{0,1:T(8,128)(2,1)}, u32[]{:S(2)}) copy-start(bf16[2560,64]{0,1:T(8,128)(2,1)} %param.15) | copy-start | bytes 983044
  55.1 23.6 %copy-start.2 = (bf16[1024,2304]{1,0:T(8,128)(2,1)S(1)}, bf16[1024,2304]{1,0:T(8,128)(2,1)}, u32[]{:S(2)}) copy-start(bf16[1024,2304]{1,0:T(8,128)(2,1)} %get-tuple-element.11.WC) | copy-start | bytes 14155780
  55.1 23.6 %copy-start.3 = (bf16[64,2560]{1,0:T(8,128)(2,1)S(1)}, bf16[64,2560]{1,0:T(8,128)(2,1)}, u32[]{:S(2)}) copy-start(bf16[64,2560]{1,0:T(8,128)(2,1)} %resid_ref.1) | copy-start | bytes 983044
  55.1 94.0 %copy-start.1 = (bf16[2560,64]{0,1:T(8,128)(2,1)S(1)}, bf16[2560,64]{0,1:T(8,128)(2,1)}, u32[]{:S(2)}) copy-start(bf16[2560,64]{0,1:T(8,128)(2,1)} %param.15) | copy-start | bytes 983044

commit v4 on v3

--- a/solution.py
+++ b/solution.py
@@ -38,11 +38,19 @@
                                         device_id={"ep": dev}, device_id_type=pl.DeviceIdType.MESH)
 
 
-def entry_barrier(devs):
+def entry_signal(devs):
     barrier = pltpu.get_barrier_semaphore()
     for dev in devs:
         pl.semaphore_signal(barrier, inc=1, device_id={"ep": dev}, device_id_type=pl.DeviceIdType.MESH)
-    pl.semaphore_wait(barrier, len(devs))
+
+
+def entry_wait(count):
+    pl.semaphore_wait(pltpu.get_barrier_semaphore(), count)
+
+
+def entry_barrier(devs):
+    entry_signal(devs)
+    entry_wait(len(devs))
 
 
 def cond(static, pred, fn):
@@ -63,8 +71,8 @@
         c.wait()
 
 
-def gather_kernel(dm, b_ref, info_ref, sw1, sw3, XG, WC, HS, TE,
-                  X, PG, I, SLT, GLT, SACC, WS, lsem, wsem, xs_ring, xr_ring, xs_d2d, xr_d2d, is_ring, ir_ring, is_d2d, ir_d2d, p_s, p_r):
+def gather_kernel(dm, resid_ref, gain_ref, router_ref, ids_ref, prio_ref, sw1, sw3, X, PG, WC, HS, TE,
+                  B, I, SLT, GLT, SACC, WS, wsem, xs_other, xr_other, xs_ring, xr_ring, xs_d2d, xr_d2d, is_ring, ir_ring, is_d2d, ir_d2d, p_s, p_r):
     n = dm.n_chip
     hops = n // 2
     tok = dm.tok
@@ -83,7 +91,7 @@
 
     def shared_stage(t):
         wait(shared_copies(t))
-        x = b_ref[t]
+        x = B[t]
         for m in range(2):
             for c in range(sff // KC):
                 dst = pl.ds(m * sff + c * KC, KC)
@@ -97,17 +105,39 @@
 
     for t in range(2):
         start(shared_copies(t))
-    entry_barrier((partner, down, up))
-
+    entry_signal((partner, down, up))
+
+    resid32 = resid_ref[...].astype(F32)
+    inv_rms = lax.rsqrt(jnp.mean(resid32 * resid32, axis=1, keepdims=True) + NORM_EPS)
+    normed = (resid32 * inv_rms * gain_ref[...]).astype(BF16)
+    for j in range(nj):
+        B[j] = normed[:, j * KC:(j + 1) * KC]
+        X[j, chip, half, :] = normed[:, j * KC:(j + 1) * KC]
+    logits = lax.dot_general(router_ref[...], normed, (((1,), (1,)), ((), ())), preferred_element_type=F32)
+    powers = jnp.exp(logits - jnp.max(logits, axis=0, keepdims=True))
+    probs = powers / jnp.sum(powers, axis=0, keepdims=True)
+    experts = lax.broadcasted_iota(jnp.int32, probs.shape, 0)
+    ids = ids_ref[...]
+
+    def put(i, k, row):
+        zero = jnp.zeros((1, tok), F32)
+        I[chip, core, pl.ds(i * KPAD + k, 1), :] = jnp.where(core == 0, jnp.concatenate([row, zero], axis=1), jnp.concatenate([zero, row], axis=1))
+
+    for k in range(KPAD):
+        if k < dm.top_k:
+            put(0, k, ids[k:k + 1].astype(F32))
+            put(1, k, prio_ref[k:k + 1, :].astype(F32))
+            put(2, k, ROUTE_SCALE * jnp.sum(jnp.where(experts == ids[k:k + 1], probs, 0.0), axis=0, keepdims=True))
+        else:
+            put(0, k, jnp.full((1, tok), -1.0, F32))
+            put(1, k, jnp.zeros((1, tok), F32))
+            put(2, k, jnp.zeros((1, tok), F32))
+
+    entry_wait(3)
     own_x = X.at[:, chip, half, :]
     own_i = I.at[chip, core]
-    first = [rcopy(b_ref, own_x, p_s.at[0], p_r.at[0], partner), rcopy(info_ref, own_i, p_s.at[1], p_r.at[1], partner)]
+    first = [rcopy(own_i, own_i, p_s.at[1], p_r.at[1], partner), rcopy(own_x, own_x, p_s.at[0], p_r.at[0], partner)]
     start(first)
-    local = [pltpu.make_async_copy(b_ref, own_x, lsem.at[0]), pltpu.make_async_copy(info_ref, own_i, lsem.at[1])]
-    start(local)
-    wait(local)
-    for c in first:
-        c.wait_recv()
 
     def x_block(j, h, rows_half):
         return X.at[j, at(-h), half, :] if rows_half else X.at[j, at(-h)]
@@ -128,8 +158,16 @@
         blk = X.at[j, at(h), pl.ds(pl.multiple_of((1 - core) * tok, tok), tok), :] if h == hops else X.at[j, at(h)]
         return rcopy(blk, blk, xs_d2d.at[h - 1, j], xr_d2d.at[h - 1, j], partner)
 
+    def x_part(j, h, other):
+        rows = pl.ds(pl.multiple_of((1 - core) * tok, tok), tok) if other else half
+        blk = X.at[j, at(-h), rows, :]
+        return rcopy(blk, blk, xs_other.at[j], xr_other.at[j], down) if other else rcopy(blk, blk, xs_ring.at[0, j], xr_ring.at[0, j], down)
+
     def forward(h, j):
-        if h > 0:
+        if h == 1:
+            x_part(j, 1, False).wait_recv()
+            x_part(j, 1, True).wait_recv()
+        elif h > 1:
             x_ring_in(j, h).wait_recv()
         if h < hops:
             x_ring(j, h).start()
@@ -150,12 +188,18 @@
             blk = i_block(h, h == hops)
             rcopy(blk, blk, is_d2d.at[h - 1], ir_d2d.at[h - 1], partner).start()
 
+    for j in range(nj // 2):
+        x_part(j, 0, False).start()
+    first[0].wait_recv()
     comm_info(0)
+    for j in range(nj // 2, nj):
+        x_part(j, 0, False).start()
+    first[1].wait_recv()
     for j in range(nj // 2):
-        forward(0, j)
+        x_part(j, 0, True).start()
     comm_info(1)
     for j in range(nj // 2, nj):
-        forward(0, j)
+        x_part(j, 0, True).start()
     for j in range(3):
         forward(1, j)
     shared_stage(0)
@@ -270,28 +314,18 @@
         g = SACC[:, pl.ds(sff + c * KC, KC)]
         HS[:, pl.ds(c * KC, KC)] = (jax.nn.silu(a) * g).astype(BF16)
 
-    def pick(j):
+    def last_hop(j, carry):
+        forward(hops, j)
+        return carry
+
+    lax.fori_loop(0, nj, last_hop, 0)
+
+    def arrive(j, carry):
         for h in range(1, hops + 1):
             x_d2d_in(j, h).wait_recv()
-        XG[:, pl.ds(pl.multiple_of(j * KC, KC), KC)] = dot(PG[...], X[j].reshape(group, KC)).astype(BF16)
-
-    lag = 3
-    for j in range(lag):
-        forward(hops, j)
-
-    def last_hop(j, carry):
-        forward(hops, j)
-        pick(j - lag)
         return carry
 
-    lax.fori_loop(lag, nj, last_hop, 0)
-
-    def last_pick(j, carry):
-        pick(j)
-        return carry
-
-    lax.fori_loop(nj - lag, nj, last_pick, 0)
-
+    lax.fori_loop(0, nj, arrive, 0)
     for c in first:
         c.wait_send()
     for h in range(hops):
@@ -301,29 +335,58 @@
         rcopy(blk, blk, is_d2d.at[h], ir_d2d.at[h], partner).wait_send()
 
     def drain(j, carry):
+        x_part(j, 0, False).wait_send()
+        x_part(j, 0, True).wait_send()
         for h in range(hops):
-            x_ring(j, h).wait_send()
+            if h > 0:
+                x_ring(j, h).wait_send()
             x_d2d(j, h + 1).wait_send()
         return carry
 
     lax.fori_loop(0, nj, drain, 0)
 
 
-def up_kernel(dm, te_ref, xg_ref, w1_ref, w3_ref, h_ref):
+def up_kernel(dm, te_ref, x_ref, pg_ref, w1, w3, h_ref, xg_ref, w_ref, wsem):
     n_tiles = dm.slots // TILE
-    for i in range(n_tiles):
-        rows = pl.ds(i * TILE, TILE)
-
-        @pl.when(i < te_ref[n_tiles])
+    nt = dm.ff // KC
+
+    def copies(c, slot):
+        cols = pl.ds(pl.multiple_of(c * KC, KC), KC)
+        return [pltpu.make_async_copy(src.at[:, :, cols], w_ref.at[slot, m], wsem.at[slot, m]) for m, src in enumerate((w1, w3))]
+
+    start(copies(0, 0))
+    start(copies(1, 1))
+
+    def pick(j, carry):
+        xg_ref[:, pl.ds(pl.multiple_of(j * KC, KC), KC)] = dot(pg_ref[...], x_ref[j].reshape(pg_ref.shape[1], KC)).astype(BF16)
+        return carry
+
+    lax.fori_loop(0, dm.nj, pick, 0)
+
+    def column(c, carry):
+        slot = c % 2
+        cols = pl.ds(pl.multiple_of(c * KC, KC), KC)
+        wait(copies(c, slot))
+        for i in range(n_tiles):
+            rows = pl.ds(i * TILE, TILE)
+
+            @pl.when(i < te_ref[n_tiles])
+            def _():
+                e = te_ref[i]
+                a = dot(xg_ref[rows, :], w_ref[slot, 0, e])
+                g = dot(xg_ref[rows, :], w_ref[slot, 1, e])
+                h_ref[rows, cols] = (jax.nn.silu(a) * g).astype(BF16)
+
+            @pl.when(i >= te_ref[n_tiles])
+            def _():
+                h_ref[rows, cols] = jnp.zeros((TILE, KC), BF16)
+
+        @pl.when(c + 2 < nt)
         def _():
-            e = te_ref[i]
-            a = dot(xg_ref[rows, :], w1_ref[e])
-            g = dot(xg_ref[rows, :], w3_ref[e])
-            h_ref[rows, :] = (jax.nn.silu(a) * g).astype(BF16)
-
-        @pl.when(i >= te_ref[n_tiles])
-        def _():
-            h_ref[rows, :] = jnp.zeros((TILE, KC), BF16)
+            start(copies(c + 2, slot))
+        return carry
+
+    lax.fori_loop(0, nt, column, 0)
 
 
 def down_kernel(dm, H, WC, TE, HS, resid_ref, ew2, sw2, out_ref,
@@ -342,11 +405,22 @@
 
     def down_copies(j, slot):
         cols = pl.ds(pl.multiple_of(j * KC, KC), KC)
-        return [pltpu.make_async_copy(ew2.at[:, :, cols], V2[slot], vsem.at[slot, 0]),
-                pltpu.make_async_copy(sw2.at[:, cols], S2[slot], vsem.at[slot, 1])]
+        return [pltpu.make_async_copy(ew2.at[:, :, cols], V2[slot], vsem.at[slot, 0])]
+
+    def shared_copies(j, slot):
+        cols = pl.ds(pl.multiple_of(j * KC, KC), KC)
+        return [pltpu.make_async_copy(sw2.at[:, cols], S2[slot], vsem.at[slot, 1])]
+
+    def shared_step(j, slot, more):
+        wait(shared_copies(j, slot))
+        SOUT[j] = dot(HS[...], S2[slot][...]).astype(BF16)
+        if more:
+            start(shared_copies(j + 2, slot))
 
     start(down_copies(0, 0))
     start(down_copies(1, 1))
+    start(shared_copies(0, 0))
+    start(shared_copies(1, 1))
     entry_barrier((partner, down, up))
 
     pr_off = [448, 0, 128, 256, 384]
@@ -404,6 +478,7 @@
         r_copy(j, g).start()
 
     skew = 2
+    late = nj // 2
 
     def ring(s, static):
         def ok(j):
@@ -426,11 +501,14 @@
             BIG[rows, :] = dot(WC[pl.ds(r * KC, KC), :], E3[...])
         for h in range(hops, -1, -1):
             q_copy(j, h).start()
-        SOUT[j] = dot(HS[...], S2[slot][...]).astype(BF16)
 
         @pl.when(j + 2 < nj)
         def _():
             start(down_copies(j + 2, slot))
+
+        @pl.when(j >= late)
+        def _():
+            shared_step(j - late, (slot + late) % 2, True)
 
     def down_pair(p, carry):
         for q in range(2):
@@ -440,6 +518,8 @@
     lax.fori_loop(0, nj // 2, down_pair, 0)
     for s in range(nj, nj + skew * hops + 2):
         ring(s, True)
+        if 0 <= s - late < nj:
+            shared_step(s - late, (s - late) % 2, s - late + 2 < nj)
 
     def drain(j, carry):
         for h in range(hops):
@@ -477,58 +557,39 @@
         nj, tok, ff, slots = dm.nj, dm.tok, dm.ff, dm.slots
         group = dm.n_chip * 2 * tok
 
-        resid32 = resid_in.astype(F32)
-        inv_rms = lax.rsqrt(jnp.mean(resid32 * resid32, axis=1, keepdims=True) + NORM_EPS)
-        normed = (resid32 * inv_rms * norm_gain).astype(BF16)
-        probs = jax.nn.softmax(jnp.dot(normed, router_w, preferred_element_type=F32), axis=1)
-        pick = expert_ids[:, :, None] == jnp.arange(router_w.shape[1], dtype=jnp.int32)
-        gates = ROUTE_SCALE * jnp.sum(jnp.where(pick, probs[:, None, :], 0.0), axis=2)
-        blocks = normed.reshape(tok, nj, KC).transpose(1, 0, 2)
-
-        def field(a, fill):
-            return jnp.pad(a.astype(F32).T, ((0, KPAD - dm.top_k), (0, 0)), constant_values=fill)
-
-        part = jnp.concatenate([field(expert_ids, -1.0), field(priority, 0.0), field(gates, 0.0)], axis=0)
-        core = lax.axis_index('ep') % 2
-        info = jnp.concatenate([jnp.where(core == 0, part, 0.0), jnp.where(core == 0, 0.0, part)], axis=1)
-
         vm = pl.BlockSpec(memory_space=pltpu.VMEM)
         sm = pl.BlockSpec(memory_space=pltpu.SMEM)
         hbm = pl.BlockSpec(memory_space=pltpu.HBM)
         dma = pltpu.SemaphoreType.DMA
         le = dm.local_e
-        picked, mix, shared_act, tile_e = pl.pallas_call(
+        rows_all, pick_rows, mix, shared_act, tile_e = pl.pallas_call(
             functools.partial(gather_kernel, dm),
-            out_shape=(jax.ShapeDtypeStruct((slots, dm.hidden), BF16),
+            out_shape=(jax.ShapeDtypeStruct((nj, dm.n_chip, 2 * tok, KC), BF16), jax.ShapeDtypeStruct((slots, group), BF16),
                        jax.ShapeDtypeStruct((group, 3 * slots), BF16), jax.ShapeDtypeStruct((tok, dm.sff), BF16),
                        jax.ShapeDtypeStruct((slots // TILE + 1,), jnp.int32)),
-            in_specs=[vm, vm, hbm, hbm],
-            out_specs=(vm, vm, vm, sm),
+            in_specs=[vm] * 5 + [hbm, hbm],
+            out_specs=(vm, vm, vm, vm, sm),
             scratch_shapes=[
-                pltpu.VMEM((nj, dm.n_chip, 2 * tok, KC), BF16),
-                pltpu.VMEM((slots, group), BF16),
+                pltpu.VMEM((nj, tok, KC), BF16),
                 pltpu.VMEM((dm.n_chip, 2, 3 * KPAD, 2 * tok), F32),
                 pltpu.VMEM((dm.n_chip, 2 * tok, KPAD), F32),
                 pltpu.VMEM((dm.n_chip, 2 * tok, KPAD), F32),
                 pltpu.VMEM((tok, 2 * dm.sff), F32),
                 pltpu.VMEM((2, 2, KC, dm.sff), BF16),
-                dma((2,)), dma((2, 2)),
+                dma((2, 2)), dma((nj,)), dma((nj,)),
                 dma((hops, nj)), dma((hops, nj)), dma((hops, nj)), dma((hops, nj)),
                 dma((hops,)), dma((hops,)), dma((hops,)), dma((hops,)), dma((2,)), dma((2,)),
             ],
-            compiler_params=pltpu.CompilerParams(collective_id=0, has_side_effects=True, vmem_limit_bytes=46 << 20),
-            cost_estimate=pl.CostEstimate(flops=35_000_000_000, bytes_accessed=40_000_000, transcendentals=0),
-        )(blocks, info, shared_w1, shared_w3)
+            compiler_params=pltpu.CompilerParams(collective_id=0, has_side_effects=True, vmem_limit_bytes=36 << 20),
+        )(resid_in, norm_gain.reshape(1, dm.hidden), router_w.T, expert_ids.T, priority.T, shared_w1, shared_w3)
         h_act = pl.pallas_call(
             functools.partial(up_kernel, dm),
             out_shape=jax.ShapeDtypeStruct((slots, ff), BF16),
-            grid=(ff // KC,),
-            in_specs=[sm, vm,
-                      pl.BlockSpec((le, dm.hidden, KC), lambda c: (0, 0, c)), pl.BlockSpec((le, dm.hidden, KC), lambda c: (0, 0, c))],
-            out_specs=pl.BlockSpec((slots, KC), lambda c: (0, c)),
-            compiler_params=pltpu.CompilerParams(vmem_limit_bytes=44 << 20),
-            cost_estimate=pl.CostEstimate(flops=10_000_000_000, bytes_accessed=70_000_000, transcendentals=0),
-        )(tile_e, picked, expert_w1, expert_w3)
+            in_specs=[sm, vm, vm, hbm, hbm],
+            out_specs=vm,
+            scratch_shapes=[pltpu.VMEM((slots, dm.hidden), BF16), pltpu.VMEM((2, 2, le, dm.hidden, KC), BF16), dma((2, 2))],
+            compiler_params=pltpu.CompilerParams(vmem_limit_bytes=36 << 20),
+        )(tile_e, rows_all, pick_rows, expert_w1, expert_w3)
         return pl.pallas_call(
             functools.partial(down_kernel, dm),
             out_shape=jax.ShapeDtypeStruct((tok, dm.hidden), BF16),

time: 149 us -> 142 us (0.953)
  Pallas kernels: 144 us -> 137 us
  other arithmetic: 4.09 us -> 0 us
  local copies, waits for them, and re-layouts: 0.84 us -> 4.76 us
    pallas_call x1, Pallas kernels: 50.6 us -> 46.1 us  [device_fn(): pl.pallas_call(functools.partial(gather_kernel, dm), out_shape=(jax.Shape...]
    pallas_call x1, Pallas kernels: 69.7 us -> 66.4 us  [device_fn(): pl.pallas_call(functools.partial(down_kernel, dm), out_shape=jax.ShapeDty...]
    unnamed x9 -> x11, local copies, waits for them, and re-layouts: 0.75 us -> 4.05 us
    reduce_sum x3 -> x0, other arithmetic: 2.14 us -> none  [the longest x1 1.18 us: device_fn(): jnp.mean(resid32 * resid32, axis=1, keepdims=True) + NORM_EPS]
where the time goes in v4:
time: 142 us
  Pallas kernels  137 us (96%)
  local copies, waits for them, and re-layouts  4.76 us (3%)
    pallas_call x1, Pallas kernels, device_fn(): pl.pallas_call(functools.partial(down_kernel, dm), out_shape=jax.ShapeDty...  66.4 us
    pallas_call x1, Pallas kernels, device_fn(): pl.pallas_call(functools.partial(gather_kernel, dm), out_shape=(jax.Shape...  46.1 us
    pallas_call x1, Pallas kernels, device_fn(): pl.pallas_call(functools.partial(up_kernel, dm), out_shape=jax.ShapeDtype...  24.4 us
    unnamed x11, local copies, waits for them, and re-layouts  4.05 us

profile of v4, /device:TPU:21, one launch (start us, length us, event | category | flops | bytes accessed | tf_op | source)
XLA Modules:
  0.0 141.7 jit_solution(7870504421824997832)
XLA Ops:
  0.0 0.7 reshape.3.gain_ref
  0.7 0.0 copy-start
  0.7 1.0 copy-done
  1.7 0.0 copy-start.2
  1.7 1.0 copy-done.2
  2.7 0.0 copy-start.3
  2.7 0.7 copy-done.3
  3.3 0.0 copy-start.4
  3.4 0.7 copy-done.4
  4.0 46.1 %shard_map.109 = (bf16[10,8,128,256]{3,2,1,0:T(8,128)(2,1)S(1)}, bf16[768,1024]{1,0:T(8,128)(2,1)S(1)}, bf16[1024,2304]{1,0:T(8,128)(2,1)S(1)}, bf16[64,3072]{1,0:T(8,128)(2,1)S(1)}, s32[7]{0:T(128)S(1)}) custom-call(bf16[64,2560]{1,0:T(8,128)(2,1)S(1)} %copy-done, f32[1,2560]{1,0:T(1,128)S(1)} %reshape.3.gain_ref, bf16[64,2560]{1,0:T(8,128)(2,1)S(1)} %bitcast.3, ...), custom_call_target="tpu_custom_call" | custom-call | tf_op jit(solution)/shard_map/pallas_call | solution.py:565
  50.1 0.0 copy-start.1
  50.1 24.4 %shard_map.110.H = bf16[768,1536]{1,0:T(8,128)(2,1)S(1)} custom-call(s32[7]{0:T(128)S(1)} %get-tuple-element.10.te_ref.TE, bf16[10,8,128,256]{3,2,1,0:T(8,128)(2,1)S(1)} %get-tuple-element.11.x_ref, bf16[768,1024]{1,0:T(8,128)(2,1)S(1)} %get-tuple-element.12.pg_ref, bf16[4,2560,1536]{2,1,0:T(8,128)(2,1)} %w1.1, bf16[4,2560,1536]{2,1,0:T(8,128)(2,1)} %w3.1), custom_call_target="tpu_custom_call" | custom-call | tf_op jit(solution)/shard_map/pallas_call | solution.py:585
  74.6 0.0 copy-done.1
  74.6 66.4 %shard_map.111 = bf16[64,2560]{1,0:T(8,128)(2,1)S(1)} custom-call(bf16[768,1536]{1,0:T(8,128)(2,1)S(1)} %shard_map.110.H, bf16[1024,2304]{1,0:T(8,128)(2,1)S(1)} %get-tuple-element.13.WC, s32[7]{0:T(128)S(1)} %get-tuple-element.10.te_ref.TE, bf16[64,3072]{1,0:T(8,128)(2,1)S(1)} %get-tuple-element.14.HS, bf16[64,2560]{1,0:T(8,128)(2,1)S(1)} %copy-done.1, ...), custom_call_target="tpu_custom_call" | custom-call | tf_op jit(solution)/shard_map/pallas_call | solution.py:593
  141.0 0.7 copy.13
Async XLA Ops:
  0.7 1.0 copy-start
  1.7 1.0 copy-start.2
  2.7 0.7 copy-start.3
  3.3 0.7 copy-start.4
  50.1 24.5 %copy-start.1 = (bf16[64,2560]{1,0:T(8,128)(2,1)S(1)}, bf16[64,2560]{1,0:T(8,128)(2,1)}, u32[]{:S(2)}) copy-start(bf16[64,2560]{1,0:T(8,128)(2,1)} %resid_ref.3) | copy-start | bytes 983044

commit v5 on v4

--- a/solution.py
+++ b/solution.py
@@ -71,7 +71,7 @@
         c.wait()
 
 
-def gather_kernel(dm, resid_ref, gain_ref, router_ref, ids_ref, prio_ref, sw1, sw3, X, PG, WC, HS, TE,
+def gather_kernel(dm, rows_ref, small_ref, sw1, sw3, X, PG, WC, HS, TE,
                   B, I, SLT, GLT, SACC, WS, wsem, xs_other, xr_other, xs_ring, xr_ring, xs_d2d, xr_d2d, is_ring, ir_ring, is_d2d, ir_d2d, p_s, p_r):
     n = dm.n_chip
     hops = n // 2
@@ -103,21 +103,22 @@
         if t + 2 < nj:
             start(shared_copies(t + 2))
 
+    entry_signal((partner, down, up))
     for t in range(2):
         start(shared_copies(t))
-    entry_signal((partner, down, up))
-
-    resid32 = resid_ref[...].astype(F32)
+
+    resid32 = rows_ref[pl.ds(0, tok), :].astype(F32)
     inv_rms = lax.rsqrt(jnp.mean(resid32 * resid32, axis=1, keepdims=True) + NORM_EPS)
-    normed = (resid32 * inv_rms * gain_ref[...]).astype(BF16)
+    normed = (resid32 * inv_rms * small_ref[pl.ds(0, 1), :]).astype(BF16)
     for j in range(nj):
         B[j] = normed[:, j * KC:(j + 1) * KC]
         X[j, chip, half, :] = normed[:, j * KC:(j + 1) * KC]
-    logits = lax.dot_general(router_ref[...], normed, (((1,), (1,)), ((), ())), preferred_element_type=F32)
+    logits = lax.dot_general(rows_ref[pl.ds(tok, rows_ref.shape[0] - tok), :], normed, (((1,), (1,)), ((), ())), preferred_element_type=F32)
     powers = jnp.exp(logits - jnp.max(logits, axis=0, keepdims=True))
     probs = powers / jnp.sum(powers, axis=0, keepdims=True)
-    experts = lax.broadcasted_iota(jnp.int32, probs.shape, 0)
-    ids = ids_ref[...]
+    experts = lax.broadcasted_iota(jnp.int32, probs.shape, 0).astype(F32)
+    ids = small_ref[pl.ds(1, dm.top_k), pl.ds(0, tok)]
+    prio_in = small_ref[pl.ds(1 + dm.top_k, dm.top_k), pl.ds(0, tok)]
 
     def put(i, k, row):
         zero = jnp.zeros((1, tok), F32)
@@ -125,8 +126,8 @@
 
     for k in range(KPAD):
         if k < dm.top_k:
-            put(0, k, ids[k:k + 1].astype(F32))
-            put(1, k, prio_ref[k:k + 1, :].astype(F32))
+            put(0, k, ids[k:k + 1])
+            put(1, k, prio_in[k:k + 1])
             put(2, k, ROUTE_SCALE * jnp.sum(jnp.where(experts == ids[k:k + 1], probs, 0.0), axis=0, keepdims=True))
         else:
             put(0, k, jnp.full((1, tok), -1.0, F32))
@@ -200,20 +201,27 @@
     comm_info(1)
     for j in range(nj // 2, nj):
         x_part(j, 0, True).start()
+    shared_stage(0)
+    shared_stage(1)
     for j in range(3):
         forward(1, j)
-    shared_stage(0)
     comm_info(2)
-    for j in range(3, 7):
+    shared_stage(2)
+    for j in range(3, 6):
         forward(1, j)
-    shared_stage(1)
-    for j in range(7, nj):
+    shared_stage(3)
+    for j in range(6, 8):
         forward(1, j)
     comm_info(3)
-    shared_stage(2)
-    for j in range(4):
+    shared_stage(4)
+    for j in range(8, nj):
+        forward(1, j)
+    shared_stage(5)
+    for j in range(2):
         forward(2, j)
     comm_info(hops)
+    for j in range(2, 4):
+        forward(2, j)
 
     for h in range(1, hops + 1):
         blk = i_block(h, h == hops, 1, 1 - core)
@@ -272,16 +280,18 @@
     for c in range(n):
         SLT[c] = slot_t[:, c * KPAD:(c + 1) * KPAD]
         GLT[c] = gate_t[:, c * KPAD:(c + 1) * KPAD]
+
+    for i in range(n_tiles):
+        TE[i] = tile_e[i]
+    TE[n_tiles] = bounds[dm.local_e - 1]
+
+    def pick_rows(c):
         for r in range(n_tiles):
             srow = (lax.broadcasted_iota(jnp.int32, (TILE, lanes), 0) + r * TILE).astype(F32)
             hit = jnp.zeros((TILE, lanes), F32)
             for k in range(dm.top_k):
                 hit = jnp.where(slot_of[c * KPAD + k:c * KPAD + k + 1] == srow, 1.0, hit)
             PG[pl.ds(r * TILE, TILE), pl.ds(c * lanes, lanes)] = hit.astype(BF16)
-
-    for i in range(n_tiles):
-        TE[i] = tile_e[i]
-    TE[n_tiles] = bounds[dm.local_e - 1]
 
     def combine_rows(c):
         sl = SLT[c]
@@ -299,11 +309,11 @@
 
     todo = [(2, j) for j in range(4, nj)] + [(3, j) for j in range(nj)]
     work = []
-    for t in range(max(nj - 3, n)):
-        if t < n:
-            work.append(functools.partial(combine_rows, t))
-        if t < nj - 3:
-            work.append(functools.partial(shared_stage, t + 3))
+    for t in range(n):
+        work.append(functools.partial(pick_rows, t))
+        if t < nj - 6:
+            work.append(functools.partial(shared_stage, t + 6))
+        work.append(functools.partial(combine_rows, t))
     total = len(work)
     for u, (h, j) in enumerate(todo):
         forward(h, j)
@@ -354,8 +364,9 @@
         cols = pl.ds(pl.multiple_of(c * KC, KC), KC)
         return [pltpu.make_async_copy(src.at[:, :, cols], w_ref.at[slot, m], wsem.at[slot, m]) for m, src in enumerate((w1, w3))]
 
-    start(copies(0, 0))
-    start(copies(1, 1))
+    depth = w_ref.shape[0]
+    for c in range(depth):
+        start(copies(c, c))
 
     def pick(j, carry):
         xg_ref[:, pl.ds(pl.multiple_of(j * KC, KC), KC)] = dot(pg_ref[...], x_ref[j].reshape(pg_ref.shape[1], KC)).astype(BF16)
@@ -364,7 +375,7 @@
     lax.fori_loop(0, dm.nj, pick, 0)
 
     def column(c, carry):
-        slot = c % 2
+        slot = c % depth
         cols = pl.ds(pl.multiple_of(c * KC, KC), KC)
         wait(copies(c, slot))
         for i in range(n_tiles):
@@ -381,9 +392,9 @@
             def _():
                 h_ref[rows, cols] = jnp.zeros((TILE, KC), BF16)
 
-        @pl.when(c + 2 < nt)
+        @pl.when(c + depth < nt)
         def _():
-            start(copies(c + 2, slot))
+            start(copies(c + depth, slot))
         return carry
 
     lax.fori_loop(0, nt, column, 0)
@@ -483,11 +494,12 @@
     def ring(s, static):
         def ok(j):
             return (0 <= j < nj) if static else (j >= 0)
-        for g in range(1, hops):
-            cond(static, ok(s - 1 - skew * g), functools.partial(relay, s - 1 - skew * g, g))
-        cond(static, ok(s - 1), functools.partial(relay, s - 1, 0))
-        cond(static, ok(s - 1 - skew * hops), lambda: turn(s - 1 - skew * hops))
-        cond(static, ok(s - 2 - skew * hops), lambda: finish(s - 2 - skew * hops))
+        for g in range(hops):
+            j = s - skew * (g + 1)
+            cond(static, ok(j), functools.partial(relay, j, g))
+        j = s - skew * (hops + 1)
+        cond(static, ok(j), functools.partial(turn, j))
+        cond(static, ok(j - 1), functools.partial(finish, j - 1))
 
     def down_step(j, slot):
         ring(j, False)
@@ -516,7 +528,7 @@
         return carry
 
     lax.fori_loop(0, nj // 2, down_pair, 0)
-    for s in range(nj, nj + skew * hops + 2):
+    for s in range(nj, nj + skew * (hops + 1) + 1):
         ring(s, True)
         if 0 <= s - late < nj:
             shared_step(s - late, (s - late) % 2, s - late + 2 < nj)
@@ -562,12 +574,18 @@
         hbm = pl.BlockSpec(memory_space=pltpu.HBM)
         dma = pltpu.SemaphoreType.DMA
         le = dm.local_e
+        rows_in = jnp.concatenate([resid_in, router_w.T], axis=0)
+
+        def wide(a):
+            return jnp.pad(a.T.astype(F32), ((0, 0), (0, dm.hidden - tok)))
+
+        small_in = jnp.concatenate([norm_gain.reshape(1, dm.hidden), wide(expert_ids), wide(priority)], axis=0)
         rows_all, pick_rows, mix, shared_act, tile_e = pl.pallas_call(
             functools.partial(gather_kernel, dm),
             out_shape=(jax.ShapeDtypeStruct((nj, dm.n_chip, 2 * tok, KC), BF16), jax.ShapeDtypeStruct((slots, group), BF16),
                        jax.ShapeDtypeStruct((group, 3 * slots), BF16), jax.ShapeDtypeStruct((tok, dm.sff), BF16),
                        jax.ShapeDtypeStruct((slots // TILE + 1,), jnp.int32)),
-            in_specs=[vm] * 5 + [hbm, hbm],
+            in_specs=[vm, vm, hbm, hbm],
             out_specs=(vm, vm, vm, vm, sm),
             scratch_shapes=[
                 pltpu.VMEM((nj, tok, KC), BF16),
@@ -581,14 +599,14 @@
                 dma((hops,)), dma((hops,)), dma((hops,)), dma((hops,)), dma((2,)), dma((2,)),
             ],
             compiler_params=pltpu.CompilerParams(collective_id=0, has_side_effects=True, vmem_limit_bytes=36 << 20),
-        )(resid_in, norm_gain.reshape(1, dm.hidden), router_w.T, expert_ids.T, priority.T, shared_w1, shared_w3)
+        )(rows_in, small_in, shared_w1, shared_w3)
         h_act = pl.pallas_call(
             functools.partial(up_kernel, dm),
             out_shape=jax.ShapeDtypeStruct((slots, ff), BF16),
             in_specs=[sm, vm, vm, hbm, hbm],
             out_specs=vm,
-            scratch_shapes=[pltpu.VMEM((slots, dm.hidden), BF16), pltpu.VMEM((2, 2, le, dm.hidden, KC), BF16), dma((2, 2))],
-            compiler_params=pltpu.CompilerParams(vmem_limit_bytes=36 << 20),
+            scratch_shapes=[pltpu.VMEM((slots, dm.hidden), BF16), pltpu.VMEM((3, 2, le, dm.hidden, KC), BF16), dma((3, 2))],
+            compiler_params=pltpu.CompilerParams(vmem_limit_bytes=40 << 20),
         )(tile_e, rows_all, pick_rows, expert_w1, expert_w3)
         return pl.pallas_call(
             functools.partial(down_kernel, dm),

time: 142 us -> 133 us (0.937)
  Pallas kernels: 137 us -> 130 us
  local copies, waits for them, and re-layouts: 4.76 us -> 1.45 us
  other arithmetic: 0 us -> 1.84 us
    pallas_call x1, Pallas kernels: 46.1 us -> 41.7 us  [device_fn(): pl.pallas_call(functools.partial(gather_kernel, dm), out_shape=(jax.Shape...]
    unnamed x11 -> x3, local copies, waits for them, and re-layouts: 4.05 us -> 0.73 us
    pallas_call x1, Pallas kernels: 24.4 us -> 22.2 us  [device_fn(): pl.pallas_call(functools.partial(up_kernel, dm), out_shape=jax.ShapeDtype...]
where the time goes in v5:
time: 133 us
  Pallas kernels  130 us (98%)
  other arithmetic  1.84 us (1%)
  local copies, waits for them, and re-layouts  1.45 us (1%)
    pallas_call x1, Pallas kernels, device_fn(): pl.pallas_call(functools.partial(down_kernel, dm), out_shape=jax.ShapeDty...  65.6 us
    pallas_call x1, Pallas kernels, device_fn(): pl.pallas_call(functools.partial(gather_kernel, dm), out_shape=(jax.Shape...  41.7 us
    pallas_call x1, Pallas kernels, device_fn(): pl.pallas_call(functools.partial(up_kernel, dm), out_shape=jax.ShapeDtype...  22.2 us

profile of v5, /device:TPU:21, one launch (start us, length us, event | category | flops | bytes accessed | tf_op | source)
XLA Modules:
  0.0 132.8 jit_solution(15947808396564728321)
XLA Ops:
  0.0 0.7 convert_bitcast_fusion
  0.7 0.7 reshape.3
  1.4 1.1 pad_maximum_fusion.rows_ref
  2.6 41.7 %shard_map.109 = (bf16[10,8,128,256]{3,2,1,0:T(8,128)(2,1)S(1)}, bf16[768,1024]{1,0:T(8,128)(2,1)S(1)}, bf16[1024,2304]{1,0:T(8,128)(2,1)S(1)}, bf16[64,3072]{1,0:T(8,128)(2,1)S(1)}, s32[7]{0:T(128)S(1)}) custom-call(bf16[128,2560]{1,0:T(8,128)(2,1)S(1)} %pad_maximum_fusion.rows_ref, f32[13,2560]{1,0:T(8,128)S(1)} %select_maximum_fusion.small_ref, ...), custom_call_target="tpu_custom_call" | custom-call | tf_op jit(solution)/shard_map/pallas_call | solution.py:583
  44.3 0.0 copy-start
  44.3 22.2 %shard_map.110.H = bf16[768,1536]{1,0:T(8,128)(2,1)S(1)} custom-call(s32[7]{0:T(128)S(1)} %get-tuple-element.10.te_ref.TE, bf16[10,8,128,256]{3,2,1,0:T(8,128)(2,1)S(1)} %get-tuple-element.11.x_ref, bf16[768,1024]{1,0:T(8,128)(2,1)S(1)} %get-tuple-element.12.pg_ref, bf16[4,2560,1536]{2,1,0:T(8,128)(2,1)} %w1.1, bf16[4,2560,1536]{2,1,0:T(8,128)(2,1)} %w3.1), custom_call_target="tpu_custom_call" | custom-call | tf_op jit(solution)/shard_map/pallas_call | solution.py:603
  66.5 0.0 copy-done
  66.5 65.6 %shard_map.111 = bf16[64,2560]{1,0:T(8,128)(2,1)S(1)} custom-call(bf16[768,1536]{1,0:T(8,128)(2,1)S(1)} %shard_map.110.H, bf16[1024,2304]{1,0:T(8,128)(2,1)S(1)} %get-tuple-element.13.WC, s32[7]{0:T(128)S(1)} %get-tuple-element.10.te_ref.TE, bf16[64,3072]{1,0:T(8,128)(2,1)S(1)} %get-tuple-element.14.HS, bf16[64,2560]{1,0:T(8,128)(2,1)S(1)} %copy-done, ...), custom_call_target="tpu_custom_call" | custom-call | tf_op jit(solution)/shard_map/pallas_call | solution.py:611
  132.1 0.7 copy.13
  (1 shorter events, 0.0 us)
Async XLA Ops:
  44.3 22.2 %copy-start = (bf16[64,2560]{1,0:T(8,128)(2,1)S(1)}, bf16[64,2560]{1,0:T(8,128)(2,1)}, u32[]{:S(2)}) copy-start(bf16[64,2560]{1,0:T(8,128)(2,1)} %resid_ref.1) | copy-start | bytes 983044

commit v6 on v5

--- a/solution.py
+++ b/solution.py
@@ -430,8 +430,6 @@
 
     start(down_copies(0, 0))
     start(down_copies(1, 1))
-    start(shared_copies(0, 0))
-    start(shared_copies(1, 1))
     entry_barrier((partner, down, up))
 
     pr_off = [448, 0, 128, 256, 384]
@@ -518,6 +516,11 @@
         def _():
             start(down_copies(j + 2, slot))
 
+        @pl.when(j == 0)
+        def _():
+            start(shared_copies(0, 0))
+            start(shared_copies(1, 1))
+
         @pl.when(j >= late)
         def _():
             shared_step(j - late, (slot + late) % 2, True)
@@ -576,10 +579,14 @@
         le = dm.local_e
         rows_in = jnp.concatenate([resid_in, router_w.T], axis=0)
 
-        def wide(a):
-            return jnp.pad(a.T.astype(F32), ((0, 0), (0, dm.hidden - tok)))
-
-        small_in = jnp.concatenate([norm_gain.reshape(1, dm.hidden), wide(expert_ids), wide(priority)], axis=0)
+        n_small = 1 + 2 * dm.top_k
+
+        def wide(a, first):
+            return lax.pad(a.T, jnp.int32(0), ((first, n_small - first - dm.top_k, 0), (0, dm.hidden - tok, 0)))
+
+        gain_rows = lax.broadcast_in_dim(norm_gain, (n_small, dm.hidden), (1,))
+        is_gain = lax.broadcasted_iota(jnp.int32, (n_small, dm.hidden), 0) == 0
+        small_in = jnp.where(is_gain, gain_rows, (wide(expert_ids, 1) + wide(priority, 1 + dm.top_k)).astype(F32))
         rows_all, pick_rows, mix, shared_act, tile_e = pl.pallas_call(
             functools.partial(gather_kernel, dm),
             out_shape=(jax.ShapeDtypeStruct((nj, dm.n_chip, 2 * tok, KC), BF16), jax.ShapeDtypeStruct((slots, group), BF16),

time: 133 us -> 132 us (level)
  no operation moved by 1% of the time
where the time goes in v6:
time: 132 us
  Pallas kernels  130 us (98%)
  other arithmetic  1.94 us (1%)
    pallas_call x1, Pallas kernels, device_fn(): pl.pallas_call(functools.partial(down_kernel, dm), out_shape=jax.ShapeDty...  65.6 us
    pallas_call x1, Pallas kernels, device_fn(): pl.pallas_call(functools.partial(gather_kernel, dm), out_shape=(jax.Shape...  41.7 us
    pallas_call x1, Pallas kernels, device_fn(): pl.pallas_call(functools.partial(up_kernel, dm), out_shape=jax.ShapeDtype...  22.2 us

profile of v6, /device:TPU:21, one launch (start us, length us, event | category | flops | bytes accessed | tf_op | source)
XLA Modules:
  0.0 132.3 jit_solution(5084298173249615552)
XLA Ops:
  0.0 0.8 convert_select_fusion.small_ref
  0.8 1.1 pad_maximum_fusion.rows_ref
  2.0 41.7 %shard_map.109 = (bf16[10,8,128,256]{3,2,1,0:T(8,128)(2,1)S(1)}, bf16[768,1024]{1,0:T(8,128)(2,1)S(1)}, bf16[1024,2304]{1,0:T(8,128)(2,1)S(1)}, bf16[64,3072]{1,0:T(8,128)(2,1)S(1)}, s32[7]{0:T(128)S(1)}) custom-call(bf16[128,2560]{1,0:T(8,128)(2,1)S(1)} %pad_maximum_fusion.rows_ref, f32[13,2560]{1,0:T(8,128)S(1)} %convert_select_fusion.small_ref, ...), custom_call_target="tpu_custom_call" | custom-call | tf_op jit(solution)/shard_map/pallas_call | solution.py:590
  43.7 0.0 copy-start
  43.7 22.2 %shard_map.110.H = bf16[768,1536]{1,0:T(8,128)(2,1)S(1)} custom-call(s32[7]{0:T(128)S(1)} %get-tuple-element.10.te_ref.TE, bf16[10,8,128,256]{3,2,1,0:T(8,128)(2,1)S(1)} %get-tuple-element.11.x_ref, bf16[768,1024]{1,0:T(8,128)(2,1)S(1)} %get-tuple-element.12.pg_ref, bf16[4,2560,1536]{2,1,0:T(8,128)(2,1)} %w1.1, bf16[4,2560,1536]{2,1,0:T(8,128)(2,1)} %w3.1), custom_call_target="tpu_custom_call" | custom-call | tf_op jit(solution)/shard_map/pallas_call | solution.py:610
  65.9 0.0 copy-done
  65.9 65.6 %shard_map.111 = bf16[64,2560]{1,0:T(8,128)(2,1)S(1)} custom-call(bf16[768,1536]{1,0:T(8,128)(2,1)S(1)} %shard_map.110.H, bf16[1024,2304]{1,0:T(8,128)(2,1)S(1)} %get-tuple-element.13.WC, s32[7]{0:T(128)S(1)} %get-tuple-element.10.te_ref.TE, bf16[64,3072]{1,0:T(8,128)(2,1)S(1)} %get-tuple-element.14.HS, bf16[64,2560]{1,0:T(8,128)(2,1)S(1)} %copy-done, ...), custom_call_target="tpu_custom_call" | custom-call | tf_op jit(solution)/shard_map/pallas_call | solution.py:618
  131.5 0.7 copy.13
  (1 shorter events, 0.0 us)
Async XLA Ops:
  43.7 22.2 %copy-start = (bf16[64,2560]{1,0:T(8,128)(2,1)S(1)}, bf16[64,2560]{1,0:T(8,128)(2,1)}, u32[]{:S(2)}) copy-start(bf16[64,2560]{1,0:T(8,128)(2,1)} %resid_ref.1) | copy-start | bytes 983044
